TPU v7x, 32 devices: a whole 2x2x4 slice. The times are simulated.
32 devices in a mesh: slab: 2 (over x), grp: 16 (over z, y, core).
Axes of the slice: x: 2, y: 2, z: 4, core: 2. Of those that a mesh axis runs over, the one named last changes fastest.
Arguments:
- blocks: bfloat16 [128, 9, 256, 256], P(('slab', 'grp')), may hold values from -0.75 to 0.75
- diag_shift: float32 [32768], P(('slab', 'grp')), may hold values from 1 to 16
- offsets: int32 [128, 2], P(('slab', 'grp')), may hold values from 0 to 4
Outputs:
- factors: bfloat16 [128, 9, 256, 256], P(('slab', 'grp'))
Inputs may be any that keep to these rules, and one draw needn't show every extreme that they name: offsets[i, 0] bounds from above the pattern's blocks left of the diagonal block of block row i and offsets[i, 1] those right of it; blocks that would lie outside the matrix are not in the pattern.
All inputs are finite; a program needn't handle non-finite values.
Results may differ from a plain program's by a relative error of at most 0.001.
Values may be sent and summed in bfloat16 or wider, within the bound.
A program may use at most 256 MiB of HBM per device.

v0:
```python
import functools

import jax
import jax.numpy as jnp
from jax import lax
from jax.experimental import pallas as pl
from jax.experimental.pallas import tpu as pltpu
from jax.sharding import PartitionSpec as P

MESH = pl.DeviceIdType.MESH
F32 = jnp.float32
BF16 = jnp.bfloat16

DIAG, SHIFT, UPPER, LOWER, SENT = 0, 1, 2, 8, 8


def kernel(
    slabs, groups, reach,
    blocks, shifts, offsets, f2,
    blk, relay, shift_own, aux_own, aux_prev, aux_next, scale, a, w1, w2, low2, h1,
    load_sem, aux_load_sem, aux_send, aux_recv, send1, recv1, send2, recv2, relay_send, relay_recv,
):
    rows, band, size, _ = blk.shape
    slab, grp = lax.axis_index("slab"), lax.axis_index("grp")
    here = slab * groups + grp
    has_prev = here > 0
    has_next = here < slabs * groups - 1
    after = lax.rem(here + 1, slabs * groups)
    before = lax.rem(here + slabs * groups - 1, slabs * groups)
    nxt = (lax.div(after, groups), lax.rem(after, groups))
    prv = (lax.div(before, groups), lax.rem(before, groups))
    inner = grp < groups - 1
    edge = jnp.logical_and(grp == groups - 1, has_next)

    half = size // 2

    def pieces(src, dst, send, recv):
        top, low = pl.ds(0, half), pl.ds(half, half)
        cuts = ((0, top), (0, low, low), (pl.ds(1, reach - 2),), (reach - 1,), (reach,))
        return [
            pltpu.make_async_remote_copy(
                src_ref=src.at[cut], dst_ref=dst.at[cut],
                send_sem=send.at[n], recv_sem=recv.at[n],
                device_id=nxt, device_id_type=MESH,
            )
            for n, cut in enumerate(cuts)
        ]

    first, last = grp == 0, grp == groups - 1
    slab_above, slab_below = slab > 0, slab < slabs - 1
    by_last = jnp.logical_and(last, slab_above)
    by_first = jnp.logical_and(first, slab_below)
    slab_after = lax.rem(slab + 1, slabs)
    slab_before = lax.rem(slab + slabs - 1, slabs)

    def relayed(t, j, src, send):
        return [
            pltpu.make_async_remote_copy(
                src_ref=src.at[reach - 1 + n], dst_ref=relay.at[t, j],
                send_sem=send.at[3 + n], recv_sem=relay_recv.at[t, j],
                device_id=device, device_id_type=MESH,
            )
            for n, device in enumerate(((slab_after, groups - 1), (slab, 0)))
        ]

    def forward(t, j):
        goal, arrived = (w2, recv2) if t else (h1, recv1)
        return [
            pltpu.make_async_remote_copy(
                src_ref=relay.at[t, j], dst_ref=goal.at[j, reach - 1 + n],
                send_sem=relay_send.at[t, j], recv_sem=arrived.at[j, 3 + n],
                device_id=device, device_id_type=MESH,
            )
            for n, device in enumerate(((slab, 0), (slab_after, 0)))
        ]

    def pass_on(t, j):
        for n, duty in enumerate((by_last, by_first)):
            @pl.when(duty)
            def _():
                copy = forward(t, j)[n]
                relayed(t, j, w2.at[0], send1.at[0])[n].wait_recv()
                copy.start()

    def start_edge(t, j, src, copies, send):
        start(relayed(t, j, src, send))
        start(copies[:3])

    def copy1(j, src):
        return pieces(src, h1.at[j], send1.at[j], recv1.at[j])

    def copy2(j, src):
        return pieces(src, w2.at[j], send2.at[j], recv2.at[j])

    def start(copies):
        for copy in copies:
            copy.start()

    def wait_send(copies):
        for copy in copies:
            copy.wait_send()

    def wait_recv(copies):
        for copy in copies:
            copy.wait_recv()

    def load(j):
        others = (pl.ds(0, reach), pl.ds(reach + 1, reach))
        return [
            pltpu.make_async_copy(blocks.at[j, cut], blk.at[j, cut], load_sem.at[j, n])
            for n, cut in enumerate(others)
        ]

    def load_diagonal(j):
        return pltpu.make_async_copy(
            blocks.at[j, reach], blk.at[j, reach], load_sem.at[j, 2]
        )

    def raw_upper(j):
        return blocks.at[j, pl.ds(reach, reach + 1)]

    aux_head = aux_own.at[:, pl.ds(0, SENT)]
    to_next = pltpu.make_async_remote_copy(
        src_ref=aux_head, dst_ref=aux_prev, send_sem=aux_send.at[0], recv_sem=aux_recv.at[0],
        device_id=nxt, device_id_type=MESH,
    )
    to_prev = pltpu.make_async_remote_copy(
        src_ref=aux_head, dst_ref=aux_next, send_sem=aux_send.at[1], recv_sem=aux_recv.at[1],
        device_id=prv, device_id_type=MESH,
    )
    shift_load = pltpu.make_async_copy(shifts, shift_own, aux_load_sem.at[0])

    shift_load.start()
    for j in range(rows):
        load_diagonal(j).start()
    for j in range(rows):
        start(load(j))

    barrier = pltpu.get_barrier_semaphore()

    @pl.when(has_prev)
    def _():
        pl.semaphore_signal(barrier, inc=1, device_id=prv, device_id_type=MESH)

    @pl.when(has_next)
    def _():
        pl.semaphore_signal(barrier, inc=1, device_id=nxt, device_id_type=MESH)

    corner = jnp.logical_and(jnp.logical_or(first, last), slabs > 1)
    partner = groups - 1 - grp

    @pl.when(corner)
    def _():
        pl.semaphore_signal(barrier, inc=1, device_id=(slab, partner), device_id_type=MESH)

    @pl.when(jnp.logical_and(corner, slab_below))
    def _():
        pl.semaphore_signal(barrier, inc=1, device_id=(slab_after, grp), device_id_type=MESH)

    @pl.when(jnp.logical_and(corner, slab_above))
    def _():
        pl.semaphore_signal(barrier, inc=1, device_id=(slab_before, grp), device_id_type=MESH)

    def count(*flags):
        return sum(flag.astype(jnp.int32) for flag in flags)

    peers = count(has_prev, has_next)
    peers = peers + count(corner) * (1 + count(slab_below, slab_above))
    pl.semaphore_wait(barrier, peers)

    row_id = lax.broadcasted_iota(jnp.int32, (size, size), 0)
    col_id = lax.broadcasted_iota(jnp.int32, (size, size), 1)
    eye = row_id == col_id

    def scale_of(values):
        positive = values > 0
        return jnp.where(positive, 1.0 / jnp.sqrt(jnp.where(positive, values, 1.0)), 0.0)

    def as_column(row):
        return jnp.sum(jnp.where(eye, row, 0.0), axis=1, keepdims=True)

    @pl.when(jnp.logical_not(has_prev))
    def _():
        aux_prev[...] = jnp.zeros_like(aux_prev)
        for j in range(reach):
            for k in range(reach + 1):
                w1[j, k] = jnp.zeros((size, size), BF16)
                w2[j, k] = jnp.zeros((size, size), BF16)

    @pl.when(jnp.logical_not(has_next))
    def _():
        aux_next[...] = jnp.zeros_like(aux_next)

    shift_load.wait()
    for j in range(rows):
        load_diagonal(j).wait()
        diagonal = jnp.sum(
            jnp.where(eye, blk[j, reach].astype(F32), 0.0), axis=0, keepdims=True
        )
        aux_own[j, DIAG : DIAG + 1, :] = shift_own[j] + diagonal
        aux_own[j, SHIFT : SHIFT + 1, :] = shift_own[j]
        row = here * rows + j
        for k in range(band):
            away = abs(k - reach)
            if k < reach:
                count = jnp.where(row - away >= 0, offsets[j, 0], 0)
            else:
                count = jnp.where(row + away < slabs * groups * rows, offsets[j, 1], 0)
            marks = jnp.where(jnp.full((1, size), count, jnp.int32) >= away, 1.0, 0.0)
            place = UPPER + k - reach if k >= reach else LOWER + k
            aux_own[j, place : place + 1, :] = marks
        if UPPER + reach + 1 < LOWER:
            spare = LOWER - UPPER - reach - 1
            aux_own[j, UPPER + reach + 1 : LOWER, :] = jnp.zeros((spare, size), F32)

    @pl.when(has_next)
    def _():
        to_next.start()

    @pl.when(has_prev)
    def _():
        to_prev.start()

    @pl.when(has_prev)
    def _():
        to_next.wait_recv()

    @pl.when(has_next)
    def _():
        to_prev.wait_recv()

    @pl.when(inner)
    def _():
        for j in reversed(range(rows)):
            start(copy1(j, raw_upper(j)))

    for j in range(rows):
        scale[j] = scale_of(aux_prev[j, DIAG : DIAG + 1, :])
        scale[rows + j] = scale_of(aux_own[j, DIAG : DIAG + 1, :])
        scale[2 * rows + j] = scale_of(aux_next[j, DIAG : DIAG + 1, :])

    def mask_of(table, j, k):
        place = UPPER + k - reach if k >= reach else LOWER + k
        return table[j, place : place + 1, :] > 0.5

    def scaled_block(block, table, j, k, shift, left, right):
        value = block.astype(F32)
        if k == reach:
            value = value + jnp.where(eye, shift, 0.0)
        value = value * left * right
        return jnp.where(mask_of(table, j, k), value, 0.0).astype(BF16)

    def scale_own(j, carry):
        for copy in load(j):
            copy.wait()
        left = as_column(scale[rows + j])
        shift = aux_own[j, SHIFT : SHIFT + 1, :]
        for k in range(band):
            value = scaled_block(blk[j, k], aux_own, j, k, shift, left, scale[j + k])
            a[j, k] = value
            if k >= reach:
                w1[reach + j, k - reach] = value
        return carry

    lax.fori_loop(0, rows, scale_own, 0)

    def update(j, low, w, put):
        def dot(x, y):
            return jnp.dot(x, y, preferred_element_type=F32)

        def partial(k):
            total = a[j, k].astype(F32)
            for m in range(1, reach + 1):
                s = k - reach + m
                if 1 <= s <= reach:
                    total = total - dot(low[j, reach - m], w[reach + j - m, s])
            return total

        def finish(k, value):
            put(k, jnp.where(mask_of(aux_own, j, k), value, 0.0).astype(BF16))

        own = w[reach + j, 0].astype(F32)
        below = row_id > col_id
        strict_low = jnp.where(below, own, 0.0).astype(BF16)
        for k in range(reach + 1, band):
            finish(k, partial(k) - dot(strict_low, w[reach + j, k - reach]))
        strict_up = jnp.where(row_id < col_id, own, 0.0).astype(BF16)
        rest = partial(reach) - dot(strict_low, strict_up)
        pivots = jnp.sum(jnp.where(eye, own, 0.0), axis=0, keepdims=True)
        finish(reach, jnp.where(below, rest / pivots, rest))
        for k in range(reach):
            m = reach - k
            pivot = w[reach + j - m, 0].astype(F32)
            strict = jnp.where(row_id < col_id, pivot, 0.0).astype(BF16)
            rest = partial(k) - dot(low[j, k], strict)
            pivots = jnp.sum(jnp.where(eye, pivot, 0.0), axis=0, keepdims=True)
            divisor = jnp.where(mask_of(aux_own, j, k), pivots, 1.0)
            finish(k, rest / divisor)

    def first_sweep(i, carry):
        j = rows - 1 - i

        @pl.when(has_prev)
        def _():
            wait_recv(copy1(j, w2.at[reach + j]))

        @pl.when(grp > 0)
        def _():
            left = as_column(scale[j])
            shift = aux_prev[j, SHIFT : SHIFT + 1, :]
            for k in range(reach + 1):
                w1[j, k] = scaled_block(
                    h1[j, k], aux_prev, j, reach + k, shift, left, scale[j + k]
                )

        @pl.when(jnp.logical_and(grp == 0, has_prev))
        def _():
            for k in range(reach + 1):
                w1[j, k] = h1[j, k]

        def put(k, value):
            if k >= reach:
                w2[reach + j, k - reach] = value
            else:
                low2[j, k] = value

        update(j, a, w1, put)

        @pl.when(inner)
        def _():
            start(copy2(j, w2.at[reach + j]))

        @pl.when(edge)
        def _():
            start_edge(0, j, w2.at[reach + j], copy1(j, w2.at[reach + j]), send1.at[j])

        return carry

    lax.fori_loop(0, rows, first_sweep, 0)

    for j in reversed(range(rows)):
        pass_on(0, j)

    def second_sweep(i, carry):
        j = rows - 1 - i

        @pl.when(has_prev)
        def _():
            wait_recv(copy2(j, w2.at[reach + j]))

        def put(k, value):
            f2[j, k] = value

        update(j, low2, w2, put)

        @pl.when(edge)
        def _():
            src = f2.at[j, pl.ds(reach, reach + 1)]
            start_edge(1, j, src, copy2(j, src), send2.at[j])

        pass_on(1, j)

        return carry

    lax.fori_loop(0, rows, second_sweep, 0)

    @pl.when(has_next)
    def _():
        to_next.wait_send()
        for j in range(rows):
            wait_send(copy1(j, w2.at[reach + j]))
            wait_send(copy2(j, w2.at[reach + j]))

    @pl.when(has_prev)
    def _():
        to_prev.wait_send()

    for n, duty in enumerate((by_last, by_first)):
        @pl.when(duty)
        def _():
            for t in range(2):
                for j in range(rows):
                    forward(t, j)[n].wait_send()


def per_device(blocks, diag_shift, offsets):
    rows, band, size, _ = blocks.shape
    reach = (band - 1) // 2
    assert rows == reach and reach <= 4
    slabs, groups = lax.axis_size("slab"), lax.axis_size("grp")
    shift = diag_shift.reshape(rows, 1, size)
    block = (size, size)
    upper = (reach + 1,) + block
    dma = pltpu.SemaphoreType.DMA
    return pl.pallas_call(
        functools.partial(kernel, slabs, groups, reach),
        out_shape=pltpu.VMEM(blocks.shape, BF16),
        in_specs=[
            pl.BlockSpec(memory_space=pltpu.HBM),
            pl.BlockSpec(memory_space=pltpu.HBM),
            pl.BlockSpec(memory_space=pltpu.SMEM),
        ],
        out_specs=pl.BlockSpec(memory_space=pltpu.VMEM),
        scratch_shapes=[
            pltpu.VMEM(blocks.shape, BF16),
            pltpu.VMEM((2, rows) + block, BF16),
            pltpu.VMEM((rows, 1, size), F32),
            pltpu.VMEM((rows, 2 * SENT, size), F32),
            pltpu.VMEM((rows, SENT, size), F32),
            pltpu.VMEM((rows, SENT, size), F32),
            pltpu.VMEM((3 * rows, 1, size), F32),
            pltpu.VMEM(blocks.shape, BF16),
            pltpu.VMEM((reach + rows,) + upper, BF16),
            pltpu.VMEM((reach + rows,) + upper, BF16),
            pltpu.VMEM((rows, reach) + block, BF16),
            pltpu.VMEM((rows,) + upper, BF16),
            dma((rows, 3)), dma((1,)), dma((2,)), dma((2,)),
            dma((rows, 5)), dma((rows, 5)), dma((rows, 5)), dma((rows, 5)),
            dma((2, rows)), dma((2, rows)),
        ],
        compiler_params=pltpu.CompilerParams(collective_id=0, has_side_effects=True, vmem_limit_bytes=57 << 20),
    )(blocks, shift, offsets)


def solution(mesh):
    return jax.shard_map(
        per_device,
        mesh=mesh,
        in_specs=(
            P(("slab", "grp"), None, None, None),
            P(("slab", "grp")),
            P(("slab", "grp"), None),
        ),
        out_specs=P(("slab", "grp"), None, None, None),
        check_vma=False,
    )
```

profile of v0, /device:TPU:8, one launch (start us, length us, event | category | flops | bytes accessed | tf_op | source)
XLA Modules:
  0.0 67.6 jit_solution(8609579670554707136)
XLA Ops:
  0.0 1.3 %copy.4.offsets = s32[4,2]{1,0:T(4,128)} copy(s32[4,2]{0,1:T(2,128)} %param.5) | data formatting | bytes 64 | tf_op args[2]
  1.3 64.1 %shard_map.37 = bf16[4,9,256,256]{3,2,1,0:T(8,128)(2,1)S(1)} custom-call(bf16[4,9,256,256]{3,2,1,0:T(8,128)(2,1)} %blocks.1, f32[4,1,256]{2,1,0:T(1,128)} %bitcast.1, s32[4,2]{1,0:T(4,128)} %copy.4.offsets), custom_call_target="tpu_custom_call" | custom-call | tf_op jit(solution)/shard_map/pallas_call | solution.py:395
  65.5 2.2 %copy.6 = bf16[4,9,256,256]{3,2,1,0:T(8,128)(2,1)} copy(bf16[4,9,256,256]{3,2,1,0:T(8,128)(2,1)S(1)} %shard_map.37) | data formatting | bytes 9437184
where the time goes:
time: 68.8 us; the launch traced here: 67.6 us
  Pallas kernels  64.1 us (93%)
  local copies, waits for them, and re-layouts  3.52 us (5%)
    pallas_call x1, Pallas kernels, per_device(): pl.pallas_call(functools.partial(kernel, slabs, groups, reach), out_shape...  64.1 us
    unnamed x2, local copies, waits for them, and re-layouts  3.52 us

commit v1 on v0

v1 whole, which is shorter than its diff:
```python
import functools

import jax
import jax.numpy as jnp
from jax import lax
from jax.experimental import pallas as pl
from jax.experimental.pallas import tpu as pltpu
from jax.sharding import PartitionSpec as P

MESH = pl.DeviceIdType.MESH
F32 = jnp.float32
BF16 = jnp.bfloat16

DIAG, SHIFT, RIGHT, LEFT, AUX = 0, 4, 8, 12, 16
PIECES = 6


def kernel(
    slabs, groups, reach,
    blocks, shifts, offsets, f2,
    blk, relay, shift_own, aux_own, aux_prev, aux_next, scale, a, w1, w2, low2, h1, acc,
    load_sem, aux_load_sem, aux_send, aux_recv, send1, recv1, send2, recv2, relay_send, relay_recv,
):
    rows, band, size, _ = blk.shape
    slab, grp = lax.axis_index("slab"), lax.axis_index("grp")
    here = slab * groups + grp
    has_prev = here > 0
    has_next = here < slabs * groups - 1
    after = lax.rem(here + 1, slabs * groups)
    before = lax.rem(here + slabs * groups - 1, slabs * groups)
    nxt = (lax.div(after, groups), lax.rem(after, groups))
    prv = (lax.div(before, groups), lax.rem(before, groups))
    inner = grp < groups - 1
    edge = jnp.logical_and(grp == groups - 1, has_next)
    from_inner = grp > 0
    from_edge = jnp.logical_and(grp == 0, has_prev)

    half = size // 2
    top, low = pl.ds(0, half), pl.ds(half, half)
    cuts = ((0, top), (0, low, low), (1,), (2,), (3,), (4,))

    first, last = grp == 0, grp == groups - 1
    slab_above, slab_below = slab > 0, slab < slabs - 1
    by_last = jnp.logical_and(last, slab_above)
    by_first = jnp.logical_and(first, slab_below)
    slab_after = lax.rem(slab + 1, slabs)
    slab_before = lax.rem(slab + slabs - 1, slabs)
    ways = ((0, 1, 2, 3), (4, 5))

    def remote(src, dst, send, recv, device):
        return pltpu.make_async_remote_copy(
            src_ref=src, dst_ref=dst, send_sem=send, recv_sem=recv,
            device_id=device, device_id_type=MESH,
        )

    def start(copies):
        for copy in copies:
            copy.start()

    def wait_send(copies):
        for copy in copies:
            copy.wait_send()

    def slot(t, j, n):
        buffer = relay.at[t, j]
        if n < 2:
            return buffer.at[cuts[n]]
        return buffer.at[n - 1 if n < 4 else n - 4]

    def edge_copies(t, j, src, send):
        return [
            remote(src.at[cuts[n]], slot(t, j, n), send.at[j, n], relay_recv.at[t, j, n], device)
            for way, device in zip(ways, ((slab_after, groups - 1), (slab, 0)))
            for n in way
        ]

    def forward(t, j, way):
        goal, arrived = (w2, recv2) if t else (w1, recv1)
        device = (slab, 0) if way == 0 else (slab_after, 0)
        return [
            remote(slot(t, j, n), goal.at[j].at[cuts[n]], relay_send.at[t, j, n], arrived.at[j, n], device)
            for n in ways[way]
        ]

    def pass_on(t, j):
        for way, duty in enumerate((by_last, by_first)):
            @pl.when(duty)
            def _():
                for n, copy in zip(ways[way], forward(t, j, way)):
                    remote(
                        slot(t, j, n), slot(t, j, n), send1.at[j, n], relay_recv.at[t, j, n], nxt
                    ).wait_recv()
                    copy.start()

    def raw_copy(j):
        return remote(
            blocks.at[j, pl.ds(reach, reach + 1)], h1.at[j], send1.at[j, 0], recv1.at[j, 0], nxt
        )

    def row_copies(w, send, recv, j, pieces):
        return [
            remote(w.at[reach + j].at[cuts[n]], w.at[j].at[cuts[n]], send.at[j, n], recv.at[j, n], nxt)
            for n in pieces
        ]

    def load(j):
        others = (pl.ds(0, reach), pl.ds(reach + 1, reach))
        return [
            pltpu.make_async_copy(blocks.at[j, cut], blk.at[j, cut], load_sem.at[j, n])
            for n, cut in enumerate(others)
        ]

    def load_diagonal(j):
        return pltpu.make_async_copy(
            blocks.at[j, reach], blk.at[j, reach], load_sem.at[j, 2]
        )

    to_next = remote(aux_own, aux_prev, aux_send.at[0], aux_recv.at[0], nxt)
    to_prev = remote(
        aux_own.at[pl.ds(0, 8)], aux_next, aux_send.at[1], aux_recv.at[1], prv
    )
    shift_load = pltpu.make_async_copy(shifts, shift_own, aux_load_sem.at[0])

    shift_load.start()
    for j in range(rows):
        load_diagonal(j).start()
    for j in range(rows):
        start(load(j))

    barrier = pltpu.get_barrier_semaphore()

    def greet(flag, device):
        @pl.when(flag)
        def _():
            pl.semaphore_signal(barrier, inc=1, device_id=device, device_id_type=MESH)

    corner = jnp.logical_and(jnp.logical_or(first, last), slabs > 1)
    greet(has_prev, prv)
    greet(has_next, nxt)
    greet(corner, (slab, groups - 1 - grp))
    greet(jnp.logical_and(corner, slab_below), (slab_after, grp))
    greet(jnp.logical_and(corner, slab_above), (slab_before, grp))

    row_id = lax.broadcasted_iota(jnp.int32, (size, size), 0)
    col_id = lax.broadcasted_iota(jnp.int32, (size, size), 1)
    eye = row_id == col_id

    def scale_of(values):
        positive = values > 0
        return jnp.where(positive, 1.0 / jnp.sqrt(jnp.where(positive, values, 1.0)), 0.0)

    def as_column(row):
        return jnp.sum(jnp.where(eye, row, 0.0), axis=1, keepdims=True)

    @pl.when(jnp.logical_not(has_prev))
    def _():
        aux_prev[...] = jnp.zeros_like(aux_prev)
        for j in range(reach):
            for k in range(reach + 1):
                w1[j, k] = jnp.zeros((size, size), BF16)
                w2[j, k] = jnp.zeros((size, size), BF16)

    @pl.when(jnp.logical_not(has_next))
    def _():
        aux_next[...] = jnp.zeros_like(aux_next)

    shift_load.wait()
    for j in range(rows):
        load_diagonal(j).wait()
        diagonal = jnp.sum(
            jnp.where(eye, blk[j, reach].astype(F32), 0.0), axis=0, keepdims=True
        )
        aux_own[DIAG + j : DIAG + j + 1, :] = shift_own[j] + diagonal
        aux_own[SHIFT + j : SHIFT + j + 1, :] = shift_own[j]
        row = here * rows + j
        right = jnp.minimum(offsets[1, j], slabs * groups * rows - 1 - row)
        left = jnp.minimum(offsets[0, j], row)
        aux_own[RIGHT + j : RIGHT + j + 1, :] = jnp.full((1, size), right, jnp.int32).astype(F32)
        aux_own[LEFT + j : LEFT + j + 1, :] = jnp.full((1, size), left, jnp.int32).astype(F32)

    def count(*flags):
        return sum(flag.astype(jnp.int32) for flag in flags)

    peers = count(has_prev, has_next)
    peers = peers + count(corner) * (1 + count(slab_below, slab_above))
    pl.semaphore_wait(barrier, peers)

    @pl.when(has_next)
    def _():
        to_next.start()

    @pl.when(has_prev)
    def _():
        to_prev.start()

    @pl.when(inner)
    def _():
        for j in reversed(range(rows)):
            raw_copy(j).start()

    @pl.when(has_prev)
    def _():
        to_next.wait_recv()

    @pl.when(has_next)
    def _():
        to_prev.wait_recv()

    for j in range(rows):
        scale[j] = scale_of(aux_prev[DIAG + j : DIAG + j + 1, :])
        scale[rows + j] = scale_of(aux_own[DIAG + j : DIAG + j + 1, :])
        scale[2 * rows + j] = scale_of(aux_next[DIAG + j : DIAG + j + 1, :])

    def mask_of(table, j, k):
        place, away = (RIGHT, k - reach) if k >= reach else (LEFT, reach - k)
        return table[pl.ds(place + j, 1), :] >= away

    def scaled_block(block, table, j, k, shift, left, right):
        value = block.astype(F32)
        if k == reach:
            value = value + jnp.where(eye, shift, 0.0)
        value = value * left * right
        if k != reach:
            value = jnp.where(mask_of(table, j, k), value, 0.0)
        return value.astype(BF16)

    def scale_own(j, carry):
        for copy in load(j):
            copy.wait()
        left = as_column(scale[rows + j])
        shift = aux_own[pl.ds(SHIFT + j, 1), :]
        for k in range(band):
            value = scaled_block(blk[j, k], aux_own, j, k, shift, left, scale[j + k])
            a[j, k] = value
            if k >= reach:
                w1[reach + j, k - reach] = value
        return carry

    lax.fori_loop(0, rows, scale_own, 0)

    below = row_id > col_id

    def dot(x, y):
        return jnp.dot(x, y, preferred_element_type=F32)

    def strict_low_of(block):
        return jnp.where(below, block.astype(F32), 0.0).astype(BF16)

    def strict_up_of(block):
        return jnp.where(row_id < col_id, block.astype(F32), 0.0).astype(BF16)

    def diagonal_of(block):
        return jnp.sum(jnp.where(eye, block.astype(F32), 0.0), axis=0, keepdims=True)

    def update(j, low, w, put, before_diagonal, after_upper, wait_piece):
        def partial(k, most):
            total = a[j, k].astype(F32)
            for m in range(1, most + 1):
                s = k - reach + m
                if 1 <= s <= reach:
                    total = total - dot(low[j, reach - m], w[reach + j - m, s])
            return total

        def finish(k, value):
            if k != reach:
                value = jnp.where(mask_of(aux_own, j, k), value, 0.0)
            put(k, value.astype(BF16))

        own = w[reach + j, 0]
        strict_low = strict_low_of(own)
        for k in range(reach + 1, band):
            finish(k, partial(k, reach) - dot(strict_low, w[reach + j, k - reach]))
        before_diagonal()
        rest = partial(reach, reach) - dot(strict_low, strict_up_of(own))
        finish(reach, jnp.where(below, rest / diagonal_of(own), rest))
        after_upper()
        for k in range(1, reach):
            acc[k - 1] = partial(k, reach - 1) - dot(low[j, k], strict_up_of(w[j + k, 0]))
        for k in range(reach):
            wait_piece(k)
            pivot = w[j + k, 0]
            if k == 0:
                rest = a[j, k].astype(F32) - dot(low[j, k], strict_up_of(pivot))
            else:
                rest = acc[k - 1] - dot(low[j, 0], w[j, k])
            divisor = jnp.where(mask_of(aux_own, j, k), diagonal_of(pivot), 1.0)
            finish(k, rest / divisor)

    def nothing(*_):
        pass

    edge_pieces = range(PIECES)
    inner_pieces = range(PIECES - 1)

    def first_sweep(i, carry):
        j = rows - 1 - i

        @pl.when(from_edge)
        def _():
            for copy in row_copies(w1, send1, recv1, j, edge_pieces):
                copy.wait_recv()

        @pl.when(from_inner)
        def _():
            raw_copy(j).wait_recv()
            left = as_column(scale[j])
            shift = aux_prev[pl.ds(SHIFT + j, 1), :]
            for k in range(reach + 1):
                w1[j, k] = scaled_block(
                    h1[j, k], aux_prev, j, reach + k, shift, left, scale[j + k]
                )
            value = w1[j, reach].astype(F32) - dot(strict_low_of(w1[j, 0]), w1[j, reach])
            w2[j, reach] = jnp.where(mask_of(aux_prev, j, 2 * reach), value, 0.0).astype(BF16)

        def put(k, value):
            if k >= reach:
                w2[reach + j, k - reach] = value
            else:
                low2[j, k] = value

        update(j, a, w1, put, nothing, nothing, nothing)

        @pl.when(inner)
        def _():
            start(row_copies(w2, send2, recv2, j, inner_pieces))

        @pl.when(edge)
        def _():
            start(edge_copies(0, j, w2.at[reach + j], send1))

        return carry

    lax.fori_loop(0, rows, first_sweep, 0)

    for j in reversed(range(rows)):
        pass_on(0, j)

    def second_sweep(i, carry):
        j = rows - 1 - i
        arrivals = row_copies(w2, send2, recv2, j, edge_pieces)

        def put(k, value):
            f2[j, k] = value

        def before_diagonal():
            @pl.when(from_edge)
            def _():
                arrivals[PIECES - 1].wait_recv()

        def after_upper():
            @pl.when(edge)
            def _():
                start(edge_copies(1, j, f2.at[j, pl.ds(reach, reach + 1)], send2))

        def wait_piece(k):
            @pl.when(has_prev)
            def _():
                if k == 0:
                    arrivals[0].wait_recv()
                arrivals[k + 1].wait_recv()

        update(j, low2, w2, put, before_diagonal, after_upper, wait_piece)
        pass_on(1, j)
        return carry

    lax.fori_loop(0, rows, second_sweep, 0)

    @pl.when(has_next)
    def _():
        to_next.wait_send()

    @pl.when(has_prev)
    def _():
        to_prev.wait_send()

    @pl.when(inner)
    def _():
        for j in range(rows):
            raw_copy(j).wait_send()
            wait_send(row_copies(w2, send2, recv2, j, inner_pieces))

    @pl.when(edge)
    def _():
        for j in range(rows):
            wait_send(edge_copies(0, j, w2.at[reach + j], send1))
            wait_send(edge_copies(1, j, f2.at[j, pl.ds(reach, reach + 1)], send2))

    for way, duty in enumerate((by_last, by_first)):
        @pl.when(duty)
        def _():
            for t in range(2):
                for j in range(rows):
                    wait_send(forward(t, j, way))


def per_device(blocks, diag_shift, offsets):
    rows, band, size, _ = blocks.shape
    reach = (band - 1) // 2
    assert rows == reach == 4
    slabs, groups = lax.axis_size("slab"), lax.axis_size("grp")
    shift = diag_shift.reshape(rows, 1, size)
    block = (size, size)
    upper = (reach + 1,) + block
    dma = pltpu.SemaphoreType.DMA
    return pl.pallas_call(
        functools.partial(kernel, slabs, groups, reach),
        out_shape=pltpu.VMEM(blocks.shape, BF16),
        in_specs=[
            pl.BlockSpec(memory_space=pltpu.HBM),
            pl.BlockSpec(memory_space=pltpu.HBM),
            pl.BlockSpec(memory_space=pltpu.SMEM),
        ],
        out_specs=pl.BlockSpec(memory_space=pltpu.VMEM),
        scratch_shapes=[
            pltpu.VMEM(blocks.shape, BF16),
            pltpu.VMEM((2, rows, 3) + block, BF16),
            pltpu.VMEM((rows, 1, size), F32),
            pltpu.VMEM((AUX, size), F32),
            pltpu.VMEM((AUX, size), F32),
            pltpu.VMEM((8, size), F32),
            pltpu.VMEM((3 * rows, 1, size), F32),
            pltpu.VMEM(blocks.shape, BF16),
            pltpu.VMEM((reach + rows,) + upper, BF16),
            pltpu.VMEM((reach + rows,) + upper, BF16),
            pltpu.VMEM((rows, reach) + block, BF16),
            pltpu.VMEM((rows,) + upper, BF16),
            pltpu.VMEM((reach - 1,) + block, F32),
            dma((rows, 3)), dma((1,)), dma((2,)), dma((2,)),
            dma((rows, PIECES)), dma((rows, PIECES)), dma((rows, PIECES)), dma((rows, PIECES)),
            dma((2, rows, PIECES)), dma((2, rows, PIECES)),
        ],
        compiler_params=pltpu.CompilerParams(collective_id=0, has_side_effects=True, vmem_limit_bytes=57 << 20),
    )(blocks, shift, offsets.T)


def solution(mesh):
    return jax.shard_map(
        per_device,
        mesh=mesh,
        in_specs=(
            P(("slab", "grp"), None, None, None),
            P(("slab", "grp")),
            P(("slab", "grp"), None),
        ),
        out_specs=P(("slab", "grp"), None, None, None),
        check_vma=False,
    )
```

time: 68.8 us -> 59 us (0.86); the launches traced: 67.6 us -> 58.9 us
  Pallas kernels: 64.1 us -> 56.7 us
  local copies, waits for them, and re-layouts: 3.52 us -> 2.19 us
    pallas_call x1, Pallas kernels: 64.1 us -> 56.7 us  [per_device(): pl.pallas_call(functools.partial(kernel, slabs, groups, reach), out_shape...]
    unnamed x2 -> x1, local copies, waits for them, and re-layouts: 3.52 us -> 2.19 us
where the time goes in v1:
time: 59 us; the launch traced here: 58.9 us
  Pallas kernels  56.7 us (96%)
  local copies, waits for them, and re-layouts  2.19 us (4%)
    pallas_call x1, Pallas kernels, per_device(): pl.pallas_call(functools.partial(kernel, slabs, groups, reach), out_shape...  56.7 us
    unnamed x1, local copies, waits for them, and re-layouts  2.19 us

profile of v1, /device:TPU:8, one launch (start us, length us, event | category | flops | bytes accessed | tf_op | source)
XLA Modules:
  0.0 58.9 jit_solution(13638473066082006123)
XLA Ops:
  0.0 56.7 %shard_map.37 = bf16[4,9,256,256]{3,2,1,0:T(8,128)(2,1)S(1)} custom-call(bf16[4,9,256,256]{3,2,1,0:T(8,128)(2,1)} %blocks.1, f32[4,1,256]{2,1,0:T(1,128)} %bitcast.2, s32[2,4]{1,0:T(2,128)} %bitcast.3), custom_call_target="tpu_custom_call" | custom-call | tf_op jit(solution)/shard_map/pallas_call | solution.py:405
  56.7 2.2 %copy.5 = bf16[4,9,256,256]{3,2,1,0:T(8,128)(2,1)} copy(bf16[4,9,256,256]{3,2,1,0:T(8,128)(2,1)S(1)} %shard_map.37) | data formatting | bytes 9437184

commit v2 on v1

--- a/solution.py
+++ b/solution.py
@@ -12,13 +12,15 @@
 BF16 = jnp.bfloat16
 
 DIAG, SHIFT, RIGHT, LEFT, AUX = 0, 4, 8, 12, 16
-PIECES = 6
+PIECES = 5
+TILE = 16
 
 
 def kernel(
     slabs, groups, reach,
     blocks, shifts, offsets, f2,
-    blk, relay, shift_own, aux_own, aux_prev, aux_next, scale, a, w1, w2, low2, h1, acc,
+    blk, relay, relay_packed, packed_out, packed_in,
+    shift_own, aux_own, aux_prev, aux_next, scale, a, w1, w2, low2, h1, acc,
     load_sem, aux_load_sem, aux_send, aux_recv, send1, recv1, send2, recv2, relay_send, relay_recv,
 ):
     rows, band, size, _ = blk.shape
@@ -36,8 +38,6 @@
     from_edge = jnp.logical_and(grp == 0, has_prev)
 
     half = size // 2
-    top, low = pl.ds(0, half), pl.ds(half, half)
-    cuts = ((0, top), (0, low, low), (1,), (2,), (3,), (4,))
 
     first, last = grp == 0, grp == groups - 1
     slab_above, slab_below = slab > 0, slab < slabs - 1
@@ -45,7 +45,7 @@
     by_first = jnp.logical_and(first, slab_below)
     slab_after = lax.rem(slab + 1, slabs)
     slab_before = lax.rem(slab + slabs - 1, slabs)
-    ways = ((0, 1, 2, 3), (4, 5))
+    ways = ((0, 1, 2), (3, 4))
 
     def remote(src, dst, send, recv, device):
         return pltpu.make_async_remote_copy(
@@ -62,23 +62,26 @@
             copy.wait_send()
 
     def slot(t, j, n):
-        buffer = relay.at[t, j]
-        if n < 2:
-            return buffer.at[cuts[n]]
-        return buffer.at[n - 1 if n < 4 else n - 4]
+        return relay_packed.at[t, j] if n == 0 else relay.at[t, j, (n - 1) % 2]
+
+    def leaving(t, j, n, src):
+        return packed_out.at[t, j] if n == 0 else src.at[n]
+
+    def landing(t, j, n):
+        return packed_in.at[t, j] if n == 0 else (w2 if t else w1).at[j, n]
 
     def edge_copies(t, j, src, send):
         return [
-            remote(src.at[cuts[n]], slot(t, j, n), send.at[j, n], relay_recv.at[t, j, n], device)
+            remote(leaving(t, j, n, src), slot(t, j, n), send.at[j, n], relay_recv.at[t, j, n], device)
             for way, device in zip(ways, ((slab_after, groups - 1), (slab, 0)))
             for n in way
         ]
 
     def forward(t, j, way):
-        goal, arrived = (w2, recv2) if t else (w1, recv1)
+        arrived = recv2 if t else recv1
         device = (slab, 0) if way == 0 else (slab_after, 0)
         return [
-            remote(slot(t, j, n), goal.at[j].at[cuts[n]], relay_send.at[t, j, n], arrived.at[j, n], device)
+            remote(slot(t, j, n), landing(t, j, n), relay_send.at[t, j, n], arrived.at[j, n], device)
             for n in ways[way]
         ]
 
@@ -97,9 +100,11 @@
             blocks.at[j, pl.ds(reach, reach + 1)], h1.at[j], send1.at[j, 0], recv1.at[j, 0], nxt
         )
 
-    def row_copies(w, send, recv, j, pieces):
+    def row_copies(t, j, pieces):
+        src = w2.at[reach + j]
+        send, recv = (send2, recv2) if t else (send1, recv1)
         return [
-            remote(w.at[reach + j].at[cuts[n]], w.at[j].at[cuts[n]], send.at[j, n], recv.at[j, n], nxt)
+            remote(leaving(0, j, n, src), landing(t, j, n), send.at[j, n], recv.at[j, n], nxt)
             for n in pieces
         ]
 
@@ -163,6 +168,17 @@
     @pl.when(jnp.logical_not(has_next))
     def _():
         aux_next[...] = jnp.zeros_like(aux_next)
+
+    def count(*flags):
+        return sum(flag.astype(jnp.int32) for flag in flags)
+
+    peers = count(has_prev, has_next)
+    peers = peers + count(corner) * (1 + count(slab_below, slab_above))
+    pl.semaphore_wait(barrier, peers)
+
+    @pl.when(inner)
+    def _():
+        raw_copy(rows - 1).start()
 
     shift_load.wait()
     for j in range(rows):
@@ -178,13 +194,6 @@
         aux_own[RIGHT + j : RIGHT + j + 1, :] = jnp.full((1, size), right, jnp.int32).astype(F32)
         aux_own[LEFT + j : LEFT + j + 1, :] = jnp.full((1, size), left, jnp.int32).astype(F32)
 
-    def count(*flags):
-        return sum(flag.astype(jnp.int32) for flag in flags)
-
-    peers = count(has_prev, has_next)
-    peers = peers + count(corner) * (1 + count(slab_below, slab_above))
-    pl.semaphore_wait(barrier, peers)
-
     @pl.when(has_next)
     def _():
         to_next.start()
@@ -195,7 +204,7 @@
 
     @pl.when(inner)
     def _():
-        for j in reversed(range(rows)):
+        for j in reversed(range(rows - 1)):
             raw_copy(j).start()
 
     @pl.when(has_prev)
@@ -251,6 +260,28 @@
 
     def diagonal_of(block):
         return jnp.sum(jnp.where(eye, block.astype(F32), 0.0), axis=0, keepdims=True)
+
+    above = lax.broadcasted_iota(jnp.int32, (half, half), 0) < lax.broadcasted_iota(jnp.int32, (half, half), 1)
+
+    def pack(t, j, block):
+        upper, corner = block[0:half, 0:half], block[half:size, half:size]
+        both = jnp.where(above, upper.astype(F32), corner.astype(F32).T)
+        packed_out[t, j, 0:half, 0:half] = both.astype(BF16)
+        packed_out[t, j, 0:half, half:size] = block[0:half, half:size]
+        packed_out[t, j, half : half + TILE, :] = jnp.broadcast_to(
+            diagonal_of(block), (TILE, size)
+        ).astype(BF16)
+
+    def unpack(t, j):
+        w = w2 if t else w1
+        both = packed_in[t, j, 0:half, 0:half].astype(F32)
+        diagonal = packed_in[t, j, half : half + TILE, :].astype(F32)[0:1]
+        on = eye[0:half, 0:half]
+        for n, part in enumerate((both, both.T)):
+            place = slice(n * half, (n + 1) * half)
+            value = jnp.where(above, part, 0.0) + jnp.where(on, diagonal[:, place], 0.0)
+            w[j, 0, place, place] = value.astype(BF16)
+        w[j, 0, 0:half, half:size] = packed_in[t, j, 0:half, half:size]
 
     def update(j, low, w, put, before_diagonal, after_upper, wait_piece):
         def partial(k, most):
@@ -297,8 +328,9 @@
 
         @pl.when(from_edge)
         def _():
-            for copy in row_copies(w1, send1, recv1, j, edge_pieces):
+            for copy in row_copies(0, j, edge_pieces):
                 copy.wait_recv()
+            unpack(0, j)
 
         @pl.when(from_inner)
         def _():
@@ -320,9 +352,13 @@
 
         update(j, a, w1, put, nothing, nothing, nothing)
 
+        @pl.when(has_next)
+        def _():
+            pack(0, j, w2[reach + j, 0])
+
         @pl.when(inner)
         def _():
-            start(row_copies(w2, send2, recv2, j, inner_pieces))
+            start(row_copies(1, j, inner_pieces))
 
         @pl.when(edge)
         def _():
@@ -337,7 +373,7 @@
 
     def second_sweep(i, carry):
         j = rows - 1 - i
-        arrivals = row_copies(w2, send2, recv2, j, edge_pieces)
+        arrivals = row_copies(1, j, edge_pieces)
 
         def put(k, value):
             f2[j, k] = value
@@ -350,14 +386,15 @@
         def after_upper():
             @pl.when(edge)
             def _():
+                pack(1, j, f2[j, reach])
                 start(edge_copies(1, j, f2.at[j, pl.ds(reach, reach + 1)], send2))
 
         def wait_piece(k):
             @pl.when(has_prev)
             def _():
+                arrivals[k].wait_recv()
                 if k == 0:
-                    arrivals[0].wait_recv()
-                arrivals[k + 1].wait_recv()
+                    unpack(1, j)
 
         update(j, low2, w2, put, before_diagonal, after_upper, wait_piece)
         pass_on(1, j)
@@ -377,7 +414,7 @@
     def _():
         for j in range(rows):
             raw_copy(j).wait_send()
-            wait_send(row_copies(w2, send2, recv2, j, inner_pieces))
+            wait_send(row_copies(1, j, inner_pieces))
 
     @pl.when(edge)
     def _():
@@ -413,7 +450,10 @@
         out_specs=pl.BlockSpec(memory_space=pltpu.VMEM),
         scratch_shapes=[
             pltpu.VMEM(blocks.shape, BF16),
-            pltpu.VMEM((2, rows, 3) + block, BF16),
+            pltpu.VMEM((2, rows, 2) + block, BF16),
+            pltpu.VMEM((2, rows, size // 2 + TILE, size), BF16),
+            pltpu.VMEM((2, rows, size // 2 + TILE, size), BF16),
+            pltpu.VMEM((2, rows, size // 2 + TILE, size), BF16),
             pltpu.VMEM((rows, 1, size), F32),
             pltpu.VMEM((AUX, size), F32),
             pltpu.VMEM((AUX, size), F32),

time: 59 us -> 57.5 us (0.975)
  Pallas kernels: 56.7 us -> 55.1 us
    pallas_call x1, Pallas kernels: 56.7 us -> 55.1 us  [per_device(): pl.pallas_call(functools.partial(kernel, slabs, groups, reach), out_shape...]
where the time goes in v2:
time: 57.5 us; the launch traced here: 57.3 us
  Pallas kernels  55.1 us (96%)
  local copies, waits for them, and re-layouts  2.19 us (4%)
    pallas_call x1, Pallas kernels, per_device(): pl.pallas_call(functools.partial(kernel, slabs, groups, reach), out_shape...  55.1 us
    unnamed x1, local copies, waits for them, and re-layouts  2.19 us

profile of v2, /device:TPU:8, one launch (start us, length us, event | category | flops | bytes accessed | tf_op | source)
XLA Modules:
  0.0 57.3 jit_solution(15653586472972613797)
XLA Ops:
  0.0 55.1 %shard_map.37 = bf16[4,9,256,256]{3,2,1,0:T(8,128)(2,1)S(1)} custom-call(bf16[4,9,256,256]{3,2,1,0:T(8,128)(2,1)} %blocks.1, f32[4,1,256]{2,1,0:T(1,128)} %bitcast.2, s32[2,4]{1,0:T(2,128)} %bitcast.3), custom_call_target="tpu_custom_call" | custom-call | tf_op jit(solution)/shard_map/pallas_call | solution.py:442
  55.1 2.2 %copy.5 = bf16[4,9,256,256]{3,2,1,0:T(8,128)(2,1)} copy(bf16[4,9,256,256]{3,2,1,0:T(8,128)(2,1)S(1)} %shard_map.37) | data formatting | bytes 9437184

commit v3 on v1

v3 whole, which is shorter than its diff:
```python
import functools

import jax
import jax.numpy as jnp
from jax import lax
from jax.experimental import pallas as pl
from jax.experimental.pallas import tpu as pltpu
from jax.sharding import PartitionSpec as P

MESH = pl.DeviceIdType.MESH
F32 = jnp.float32
BF16 = jnp.bfloat16

DIAG, SHIFT, RIGHT, LEFT, AUX = 0, 4, 8, 12, 16
TILE = 16
LOAD_FIRST, LOAD_UPPER, LOAD_LOWER, LOAD_SHIFT, LOAD_OFFSETS = range(5)


def kernel(
    slabs, groups, reach,
    blocks, shifts, offsets_in, f2,
    blk, relay, offsets, shift_own, aux_own, aux_prev, aux_next, scale, a, w1, w2, d1, d2, low2, h1, acc,
    load_sem, aux_sem, row_send, recv1, recv2, relay_recv, relay_send,
):
    rows, band, size, _ = blk.shape
    slab, grp = lax.axis_index("slab"), lax.axis_index("grp")
    here = slab * groups + grp
    has_prev = here > 0
    has_next = here < slabs * groups - 1
    after = lax.rem(here + 1, slabs * groups)
    before = lax.rem(here + slabs * groups - 1, slabs * groups)
    nxt = (lax.div(after, groups), lax.rem(after, groups))
    prv = (lax.div(before, groups), lax.rem(before, groups))
    inner = grp < groups - 1
    edge = jnp.logical_and(grp == groups - 1, has_next)
    from_inner = grp > 0
    from_edge = jnp.logical_and(grp == 0, has_prev)

    half = size // 2

    first, last = grp == 0, grp == groups - 1
    slab_above, slab_below = slab > 0, slab < slabs - 1
    by_last = jnp.logical_and(last, slab_above)
    by_first = jnp.logical_and(first, slab_below)
    slab_after = lax.rem(slab + 1, slabs)
    slab_before = lax.rem(slab + slabs - 1, slabs)
    packed = half + TILE
    tall = packed + reach * size

    def cut(n):
        return pl.ds(0, packed + size) if n == 0 else pl.ds(packed + n * size, size)

    def upper(s):
        return pl.ds(packed + (s - 1) * size, size)

    ways = ((0, 1), (2, 3))
    way_rows = (pl.ds(0, packed + 2 * size), pl.ds(0, 2 * size))

    def remote(src, dst, send, recv, device):
        return pltpu.make_async_remote_copy(
            src_ref=src, dst_ref=dst, send_sem=send, recv_sem=recv,
            device_id=device, device_id_type=MESH,
        )

    def start(copies):
        for copy in copies:
            copy.start()

    def wait_send(copies):
        for copy in copies:
            copy.wait_send()

    def only(flag, body):
        def run(_, carry):
            body()
            return carry

        lax.fori_loop(0, jnp.where(flag, 1, 0), run, 0)

    def slot(t, j, n):
        return relay.at[t, j, cut(n) if n < 2 else pl.ds((n - 2) * size, size)]

    def edge_copies(t, j):
        src, send = (w1, row_send.at[0]) if t else (w2, row_send.at[1])
        return [
            remote(src.at[reach + j, cut(n)], slot(t, j, n), send, relay_recv.at[t, j, i], device)
            for way, device in zip(ways, ((slab_after, groups - 1), (slab, 0)))
            for i, n in enumerate(way)
        ]

    def forward(t, j, way):
        device = (slab, 0) if way == 0 else (slab_after, 0)
        return [
            remote(
                slot(t, j, n), (w2 if t else w1).at[j, cut(n)], relay_send.at[0],
                recv2.at[j, n] if t else recv1.at[j, way], device,
            )
            for n in ways[way]
        ]

    def pass_on(t, j):
        for way, duty in enumerate((by_last, by_first)):
            def go():
                for i, (n, copy) in enumerate(zip(ways[way], forward(t, j, way))):
                    remote(
                        slot(t, j, n), slot(t, j, n), relay_send.at[0], relay_recv.at[t, j, i], nxt
                    ).wait_recv()
                    copy.start()

            only(duty, go)

    def raw_copy(j):
        return remote(
            blk.at[j, pl.ds(reach, reach + 1)], h1.at[j], row_send.at[0], recv1.at[j, 0], nxt
        )

    def row_copy(j, n):
        return remote(w2.at[reach + j, cut(n)], w2.at[j, cut(n)], row_send.at[1], recv2.at[j, n], nxt)

    def load(which, rows_of, cut_of):
        return pltpu.make_async_copy(
            blocks.at[rows_of, cut_of], blk.at[rows_of, cut_of], load_sem.at[which]
        )

    above_cut = pl.ds(reach, reach + 1)
    load_first = load(LOAD_FIRST, pl.ds(rows - 1, 1), above_cut)
    load_upper = load(LOAD_UPPER, pl.ds(0, rows - 1), above_cut)
    load_lower = load(LOAD_LOWER, pl.ds(0, rows), pl.ds(0, reach))
    load_shift = pltpu.make_async_copy(shifts, shift_own, load_sem.at[LOAD_SHIFT])
    load_offsets = pltpu.make_async_copy(offsets_in, offsets, load_sem.at[LOAD_OFFSETS])

    to_next = remote(aux_own, aux_prev, aux_sem.at[0], aux_sem.at[1], nxt)
    to_prev = remote(aux_own.at[pl.ds(0, 8)], aux_next, aux_sem.at[2], aux_sem.at[3], prv)

    barrier = pltpu.get_barrier_semaphore()

    def greet(flag, device):
        @pl.when(flag)
        def _():
            pl.semaphore_signal(barrier, inc=1, device_id=device, device_id_type=MESH)

    corner = jnp.logical_and(jnp.logical_or(first, last), slabs > 1)
    greet(has_prev, prv)
    greet(has_next, nxt)
    greet(corner, (slab, groups - 1 - grp))
    greet(jnp.logical_and(corner, slab_below), (slab_after, grp))
    greet(jnp.logical_and(corner, slab_above), (slab_before, grp))

    load_first.start()
    load_shift.start()
    load_offsets.start()
    load_upper.start()
    load_lower.start()

    def count(*flags):
        return sum(flag.astype(jnp.int32) for flag in flags)

    peers = count(has_prev, has_next)
    peers = peers + count(corner) * (1 + count(slab_below, slab_above))
    load_first.wait()
    pl.semaphore_wait(barrier, peers)

    @pl.when(inner)
    def _():
        raw_copy(rows - 1).start()

    row_id = lax.broadcasted_iota(jnp.int32, (size, size), 0)
    col_id = lax.broadcasted_iota(jnp.int32, (size, size), 1)
    eye = row_id == col_id

    def scale_of(values):
        positive = values > 0
        return jnp.where(positive, 1.0 / jnp.sqrt(jnp.where(positive, values, 1.0)), 0.0)

    def as_column(row):
        return jnp.sum(jnp.where(eye, row, 0.0), axis=1, keepdims=True)

    @pl.when(jnp.logical_not(has_prev))
    def _():
        aux_prev[...] = jnp.zeros_like(aux_prev)
        for w, d in ((w1, d1), (w2, d2)):
            for j in range(reach):
                w[j] = jnp.zeros((tall, size), BF16)
                d[j] = jnp.zeros((size, size), BF16)

    @pl.when(jnp.logical_not(has_next))
    def _():
        aux_next[...] = jnp.zeros_like(aux_next)

    load_shift.wait()
    load_offsets.wait()
    load_upper.wait()
    for j in range(rows):
        diagonal = jnp.sum(
            jnp.where(eye, blk[j, reach].astype(F32), 0.0), axis=0, keepdims=True
        )
        aux_own[DIAG + j : DIAG + j + 1, :] = shift_own[j] + diagonal
        aux_own[SHIFT + j : SHIFT + j + 1, :] = shift_own[j]
        row = here * rows + j
        right = jnp.minimum(offsets[1, j], slabs * groups * rows - 1 - row)
        left = jnp.minimum(offsets[0, j], row)
        aux_own[RIGHT + j : RIGHT + j + 1, :] = jnp.full((1, size), right, jnp.int32).astype(F32)
        aux_own[LEFT + j : LEFT + j + 1, :] = jnp.full((1, size), left, jnp.int32).astype(F32)

    @pl.when(has_next)
    def _():
        to_next.start()

    @pl.when(has_prev)
    def _():
        to_prev.start()

    @pl.when(inner)
    def _():
        for j in reversed(range(rows - 1)):
            raw_copy(j).start()

    @pl.when(has_prev)
    def _():
        to_next.wait_recv()

    @pl.when(has_next)
    def _():
        to_prev.wait_recv()

    for j in range(rows):
        scale[j] = scale_of(aux_prev[DIAG + j : DIAG + j + 1, :])
        scale[rows + j] = scale_of(aux_own[DIAG + j : DIAG + j + 1, :])
        scale[2 * rows + j] = scale_of(aux_next[DIAG + j : DIAG + j + 1, :])

    def mask_of(table, j, k):
        place, away = (RIGHT, k - reach) if k >= reach else (LEFT, reach - k)
        return table[pl.ds(place + j, 1), :] >= away

    def scaled_block(block, table, j, k, shift, left, right):
        value = block.astype(F32)
        if k == reach:
            value = value + jnp.where(eye, shift, 0.0)
        value = value * left * right
        if k != reach:
            value = jnp.where(mask_of(table, j, k), value, 0.0)
        return value.astype(BF16)

    def scale_own(j, carry):
        left = as_column(scale[rows + j])
        shift = aux_own[pl.ds(SHIFT + j, 1), :]
        for k in range(band):
            value = scaled_block(blk[j, k], aux_own, j, k, shift, left, scale[j + k])
            a[j, k] = value
            if k == reach:
                d1[reach + j] = value
            elif k > reach:
                w1[reach + j, upper(k - reach)] = value
        return carry

    load_lower.wait()
    lax.fori_loop(0, rows, scale_own, 0)

    below = row_id > col_id

    def dot(x, y):
        return jnp.dot(x, y, preferred_element_type=F32)

    def strict_low_of(block):
        return jnp.where(below, block.astype(F32), 0.0).astype(BF16)

    def strict_up_of(block):
        return jnp.where(row_id < col_id, block.astype(F32), 0.0).astype(BF16)

    def diagonal_of(block):
        return jnp.sum(jnp.where(eye, block.astype(F32), 0.0), axis=0, keepdims=True)

    above = lax.broadcasted_iota(jnp.int32, (half, half), 0) < lax.broadcasted_iota(jnp.int32, (half, half), 1)

    def pack(w, j, block):
        top, corner = block[0:half, 0:half], block[half:size, half:size]
        both = jnp.where(above, top.astype(F32), corner.astype(F32).T)
        w[reach + j, 0:half, 0:half] = both.astype(BF16)
        w[reach + j, 0:half, half:size] = block[0:half, half:size]
        w[reach + j, half:packed, :] = jnp.broadcast_to(diagonal_of(block), (TILE, size)).astype(BF16)

    def unpack(w, d, j):
        both = w[j, 0:half, 0:half].astype(F32)
        diagonal = w[j, half:packed, :].astype(F32)[0:1]
        on = eye[0:half, 0:half]
        for n, part in enumerate((both, both.T)):
            place = slice(n * half, (n + 1) * half)
            value = jnp.where(above, part, 0.0) + jnp.where(on, diagonal[:, place], 0.0)
            d[j, place, place] = value.astype(BF16)
        d[j, 0:half, half:size] = w[j, 0:half, half:size]

    def update(j, low, w, d, put, before_diagonal, after_upper, wait_piece):
        def partial(k, most):
            total = a[j, k].astype(F32)
            for m in range(1, most + 1):
                s = k - reach + m
                if 1 <= s <= reach:
                    total = total - dot(low[j, reach - m], w[reach + j - m, upper(s)])
            return total

        def finish(k, value):
            if k != reach:
                value = jnp.where(mask_of(aux_own, j, k), value, 0.0)
            put(k, value.astype(BF16))

        own = d[reach + j]
        strict_low = strict_low_of(own)
        for k in range(reach + 1, band):
            finish(k, partial(k, reach) - dot(strict_low, w[reach + j, upper(k - reach)]))
        before_diagonal()
        rest = partial(reach, reach) - dot(strict_low, strict_up_of(own))
        finish(reach, jnp.where(below, rest / diagonal_of(own), rest))
        after_upper()
        for k in range(1, reach):
            acc[k - 1] = partial(k, reach - 1) - dot(low[j, k], strict_up_of(d[j + k]))
        for k in range(reach):
            wait_piece(k)
            pivot = d[j + k]
            if k == 0:
                rest = a[j, k].astype(F32) - dot(low[j, k], strict_up_of(pivot))
            else:
                rest = acc[k - 1] - dot(low[j, 0], w[j, upper(k)])
            divisor = jnp.where(mask_of(aux_own, j, k), diagonal_of(pivot), 1.0)
            finish(k, rest / divisor)

    def nothing(*_):
        pass

    def first_sweep(i, carry):
        j = rows - 1 - i

        @pl.when(from_edge)
        def _():
            for way, part in enumerate(way_rows):
                remote(w1.at[j, part], w1.at[j, part], row_send.at[1], recv1.at[j, way], nxt).wait_recv()
            unpack(w1, d1, j)

        @pl.when(from_inner)
        def _():
            raw_copy(j).wait_recv()
            left = as_column(scale[j])
            shift = aux_prev[pl.ds(SHIFT + j, 1), :]
            for k in range(reach + 1):
                value = scaled_block(
                    h1[j, k], aux_prev, j, reach + k, shift, left, scale[j + k]
                )
                if k == 0:
                    d1[j] = value
                else:
                    w1[j, upper(k)] = value
            farthest = w1[j, upper(reach)]
            value = farthest.astype(F32) - dot(strict_low_of(d1[j]), farthest)
            w2[j, upper(reach)] = jnp.where(mask_of(aux_prev, j, 2 * reach), value, 0.0).astype(BF16)

        def put(k, value):
            if k == reach:
                d2[reach + j] = value
            elif k > reach:
                w2[reach + j, upper(k - reach)] = value
            else:
                low2[j, k] = value

        update(j, a, w1, d1, put, nothing, nothing, nothing)

        @pl.when(has_next)
        def _():
            pack(w2, j, d2[reach + j])

        @pl.when(inner)
        def _():
            start([row_copy(j, n) for n in range(3)])

        @pl.when(edge)
        def _():
            start(edge_copies(0, j))

        return carry

    lax.fori_loop(0, rows, first_sweep, 0)

    def pass_first(i, carry):
        pass_on(0, rows - 1 - i)
        return carry

    lax.fori_loop(0, jnp.where(jnp.logical_or(by_last, by_first), rows, 0), pass_first, 0)

    def second_sweep(i, carry):
        j = rows - 1 - i

        def put(k, value):
            f2[j, k] = value

        def before_diagonal():
            @pl.when(from_edge)
            def _():
                row_copy(j, 3).wait_recv()

        def after_upper():
            def send():
                pack(w1, j, f2[j, reach])
                for s in range(1, reach + 1):
                    w1[reach + j, upper(s)] = f2[j, reach + s]
                start(edge_copies(1, j))

            only(edge, send)
            pass_on(1, j)

        def wait_piece(k):
            if k != 1:
                @pl.when(has_prev)
                def _():
                    row_copy(j, max(k - 1, 0)).wait_recv()
                    if k == 0:
                        unpack(w2, d2, j)

        update(j, low2, w2, d2, put, before_diagonal, after_upper, wait_piece)
        return carry

    @pl.when(has_next)
    def _():
        to_next.wait_send()

    @pl.when(has_prev)
    def _():
        to_prev.wait_send()

    @pl.when(inner)
    def _():
        raw = blk.at[:, pl.ds(reach, reach + 1)]
        remote(raw, h1, row_send.at[0], recv1.at[0, 0], nxt).wait_send()

    lax.fori_loop(0, rows, second_sweep, 0)

    @pl.when(inner)
    def _():
        part = w2.at[pl.ds(reach, rows), pl.ds(0, packed + (reach - 1) * size)]
        remote(part, part, row_send.at[1], recv2.at[0, 0], nxt).wait_send()

    def sent_edge():
        for t, w in enumerate((w2, w1)):
            part = w.at[pl.ds(reach, rows)]
            remote(part, part, row_send.at[1 - t], recv2.at[0, 0], nxt).wait_send()

    only(edge, sent_edge)
    for way, duty in enumerate((by_last, by_first)):
        def passed():
            part = relay.at[:, :, way_rows[way]]
            remote(part, part, relay_send.at[0], recv2.at[0, 0], nxt).wait_send()

        only(duty, passed)


def per_device(blocks, diag_shift, offsets):
    rows, band, size, _ = blocks.shape
    reach = (band - 1) // 2
    assert rows == reach == 4
    slabs, groups = lax.axis_size("slab"), lax.axis_size("grp")
    shift = diag_shift.reshape(rows, 1, size)
    block = (size, size)
    packed = size // 2 + TILE
    tall = (reach + rows, packed + reach * size, size)
    dma = pltpu.SemaphoreType.DMA
    return pl.pallas_call(
        functools.partial(kernel, slabs, groups, reach),
        out_shape=pltpu.VMEM(blocks.shape, BF16),
        in_specs=[pl.BlockSpec(memory_space=pltpu.HBM)] * 3,
        out_specs=pl.BlockSpec(memory_space=pltpu.VMEM),
        scratch_shapes=[
            pltpu.VMEM(blocks.shape, BF16),
            pltpu.VMEM((2, rows, packed + 2 * size, size), BF16),
            pltpu.SMEM((2, rows), jnp.int32),
            pltpu.VMEM((rows, 1, size), F32),
            pltpu.VMEM((AUX, size), F32),
            pltpu.VMEM((AUX, size), F32),
            pltpu.VMEM((8, size), F32),
            pltpu.VMEM((3 * rows, 1, size), F32),
            pltpu.VMEM(blocks.shape, BF16),
            pltpu.VMEM(tall, BF16),
            pltpu.VMEM(tall, BF16),
            pltpu.VMEM((reach + rows,) + block, BF16),
            pltpu.VMEM((reach + rows,) + block, BF16),
            pltpu.VMEM((rows, reach) + block, BF16),
            pltpu.VMEM((rows, reach + 1) + block, BF16),
            pltpu.VMEM((reach - 1,) + block, F32),
            dma((5,)), dma((4,)), dma((2,)), dma((rows, 2)), dma((rows, 4)),
            dma((2, rows, 2)), dma((1,)),
        ],
        compiler_params=pltpu.CompilerParams(collective_id=0, has_side_effects=True, vmem_limit_bytes=57 << 20),
    )(blocks, shift, offsets.T)


def solution(mesh):
    return jax.shard_map(
        per_device,
        mesh=mesh,
        in_specs=(
            P(("slab", "grp"), None, None, None),
            P(("slab", "grp")),
            P(("slab", "grp"), None),
        ),
        out_specs=P(("slab", "grp"), None, None, None),
        check_vma=False,
    )
```

time: 59 us -> 55.3 us (0.937)
  Pallas kernels: 56.7 us -> 53 us
    pallas_call x1, Pallas kernels: 56.7 us -> 53 us  [per_device(): pl.pallas_call(functools.partial(kernel, slabs, groups, reach), out_shape...]
where the time goes in v3:
time: 55.3 us; the launch traced here: 55.2 us
  Pallas kernels  53 us (96%)
  local copies, waits for them, and re-layouts  2.19 us (4%)
    pallas_call x1, Pallas kernels, per_device(): pl.pallas_call(functools.partial(kernel, slabs, groups, reach), out_shape...  53 us
    unnamed x1, local copies, waits for them, and re-layouts  2.19 us

profile of v3, /device:TPU:8, one launch (start us, length us, event | category | flops | bytes accessed | tf_op | source)
XLA Modules:
  0.0 55.2 jit_solution(16776722407339945313)
XLA Ops:
  0.0 53.0 %shard_map.37 = bf16[4,9,256,256]{3,2,1,0:T(8,128)(2,1)S(1)} custom-call(bf16[4,9,256,256]{3,2,1,0:T(8,128)(2,1)} %blocks.1, f32[4,1,256]{2,1,0:T(1,128)} %bitcast.2, s32[2,4]{1,0:T(2,128)} %bitcast.3), custom_call_target="tpu_custom_call" | custom-call | tf_op jit(solution)/shard_map/pallas_call | solution.py:463
  53.0 2.2 %copy.5 = bf16[4,9,256,256]{3,2,1,0:T(8,128)(2,1)} copy(bf16[4,9,256,256]{3,2,1,0:T(8,128)(2,1)S(1)} %shard_map.37) | data formatting | bytes 9437184

commit v4 on v3

--- a/solution.py
+++ b/solution.py
@@ -12,15 +12,17 @@
 BF16 = jnp.bfloat16
 
 DIAG, SHIFT, RIGHT, LEFT, AUX = 0, 4, 8, 12, 16
-TILE = 16
+TILE = 8
 LOAD_FIRST, LOAD_UPPER, LOAD_LOWER, LOAD_SHIFT, LOAD_OFFSETS = range(5)
+SEND_RAW, SEND_NEXT, RELAYED, SEND_ROWS, SEND_PREV, SEND_ASIDE = range(6)
+SPAN = 4
 
 
 def kernel(
     slabs, groups, reach,
     blocks, shifts, offsets_in, f2,
-    blk, relay, offsets, shift_own, aux_own, aux_prev, aux_next, scale, a, w1, w2, d1, d2, low2, h1, acc,
-    load_sem, aux_sem, row_send, recv1, recv2, relay_recv, relay_send,
+    blk, relay, aside, offsets, shift_own, aux_own, aux_prev, aux_next, scale, a, w1, w2, d1, d2, low2, h1, acc,
+    sem, aux_recv, recv1, recv2, relay_recv, aside_recv,
 ):
     rows, band, size, _ = blk.shape
     slab, grp = lax.axis_index("slab"), lax.axis_index("grp")
@@ -45,15 +47,16 @@
     slab_after = lax.rem(slab + 1, slabs)
     slab_before = lax.rem(slab + slabs - 1, slabs)
     packed = half + TILE
-    tall = packed + reach * size
+    diag = reach * size
+    tall = diag + packed
 
     def cut(n):
-        return pl.ds(0, packed + size) if n == 0 else pl.ds(packed + n * size, size)
+        return pl.ds(2 * size, 2 * size + packed) if n == 0 else pl.ds((2 - n) * size, size)
 
     def upper(s):
-        return pl.ds(packed + (s - 1) * size, size)
-
-    ways = ((0, 1), (2, 3))
+        return pl.ds((reach - s) * size, size)
+
+    ways = ((0,), (1, 2))
     way_rows = (pl.ds(0, packed + 2 * size), pl.ds(0, 2 * size))
 
     def remote(src, dst, send, recv, device):
@@ -78,10 +81,10 @@
         lax.fori_loop(0, jnp.where(flag, 1, 0), run, 0)
 
     def slot(t, j, n):
-        return relay.at[t, j, cut(n) if n < 2 else pl.ds((n - 2) * size, size)]
+        return relay.at[t, j, way_rows[0] if n == 0 else pl.ds((n - 1) * size, size)]
 
     def edge_copies(t, j):
-        src, send = (w1, row_send.at[0]) if t else (w2, row_send.at[1])
+        src, send = (w1, sem.at[SEND_RAW]) if t else (w2, sem.at[SEND_ROWS])
         return [
             remote(src.at[reach + j, cut(n)], slot(t, j, n), send, relay_recv.at[t, j, i], device)
             for way, device in zip(ways, ((slab_after, groups - 1), (slab, 0)))
@@ -92,8 +95,8 @@
         device = (slab, 0) if way == 0 else (slab_after, 0)
         return [
             remote(
-                slot(t, j, n), (w2 if t else w1).at[j, cut(n)], relay_send.at[0],
-                recv2.at[j, n] if t else recv1.at[j, way], device,
+                slot(t, j, n), (w2 if t else w1).at[j, cut(n)], sem.at[RELAYED],
+                recv2.at[j, n] if t else recv1.at[j], device,
             )
             for n in ways[way]
         ]
@@ -103,7 +106,7 @@
             def go():
                 for i, (n, copy) in enumerate(zip(ways[way], forward(t, j, way))):
                     remote(
-                        slot(t, j, n), slot(t, j, n), relay_send.at[0], relay_recv.at[t, j, i], nxt
+                        slot(t, j, n), slot(t, j, n), sem.at[RELAYED], relay_recv.at[t, j, i], nxt
                     ).wait_recv()
                     copy.start()
 
@@ -111,26 +114,48 @@
 
     def raw_copy(j):
         return remote(
-            blk.at[j, pl.ds(reach, reach + 1)], h1.at[j], row_send.at[0], recv1.at[j, 0], nxt
+            blk.at[j, pl.ds(reach, reach + 1)], h1.at[j], sem.at[SEND_RAW], recv1.at[j], nxt
+        )
+
+    turns = aside.shape[0]
+    far = jnp.logical_and(lax.rem(grp, SPAN) == SPAN - 1, inner)
+    from_far = jnp.logical_and(lax.rem(grp, SPAN) == 0, grp > 0)
+    inner_near = jnp.logical_and(inner, jnp.logical_not(far))
+
+    def raw_aside():
+        turn = lax.div(grp, SPAN)
+        return remote(
+            blk.at[0, 2 * reach], aside.at[turn], sem.at[SEND_RAW], aside_recv.at[turn], (slab, 0)
+        )
+
+    def raw_straight():
+        part = pl.ds(0, reach)
+        return remote(
+            blk.at[0, pl.ds(reach, reach)], h1.at[0, part], sem.at[SEND_RAW], recv1.at[0], nxt
+        )
+
+    def help_on(turn):
+        return remote(
+            aside.at[turn], h1.at[0, reach], sem.at[SEND_ASIDE], recv1.at[0], (slab, SPAN * (turn + 1))
         )
 
     def row_copy(j, n):
-        return remote(w2.at[reach + j, cut(n)], w2.at[j, cut(n)], row_send.at[1], recv2.at[j, n], nxt)
+        return remote(w2.at[reach + j, cut(n)], w2.at[j, cut(n)], sem.at[SEND_ROWS], recv2.at[j, n], nxt)
 
     def load(which, rows_of, cut_of):
         return pltpu.make_async_copy(
-            blocks.at[rows_of, cut_of], blk.at[rows_of, cut_of], load_sem.at[which]
+            blocks.at[rows_of, cut_of], blk.at[rows_of, cut_of], sem.at[which]
         )
 
     above_cut = pl.ds(reach, reach + 1)
     load_first = load(LOAD_FIRST, pl.ds(rows - 1, 1), above_cut)
     load_upper = load(LOAD_UPPER, pl.ds(0, rows - 1), above_cut)
     load_lower = load(LOAD_LOWER, pl.ds(0, rows), pl.ds(0, reach))
-    load_shift = pltpu.make_async_copy(shifts, shift_own, load_sem.at[LOAD_SHIFT])
-    load_offsets = pltpu.make_async_copy(offsets_in, offsets, load_sem.at[LOAD_OFFSETS])
-
-    to_next = remote(aux_own, aux_prev, aux_sem.at[0], aux_sem.at[1], nxt)
-    to_prev = remote(aux_own.at[pl.ds(0, 8)], aux_next, aux_sem.at[2], aux_sem.at[3], prv)
+    load_shift = pltpu.make_async_copy(shifts, shift_own, sem.at[LOAD_SHIFT])
+    load_offsets = pltpu.make_async_copy(offsets_in, offsets, sem.at[LOAD_OFFSETS])
+
+    to_next = remote(aux_own, aux_prev, sem.at[SEND_NEXT], aux_recv.at[0], nxt)
+    to_prev = remote(aux_own.at[pl.ds(0, 8)], aux_next, sem.at[SEND_PREV], aux_recv.at[1], prv)
 
     barrier = pltpu.get_barrier_semaphore()
 
@@ -143,6 +168,9 @@
     greet(has_prev, prv)
     greet(has_next, nxt)
     greet(corner, (slab, groups - 1 - grp))
+    greet(jnp.logical_or(far, from_far), (slab, 0))
+    for turn in range(turns):
+        greet(first, (slab, SPAN * turn + SPAN - 1))
     greet(jnp.logical_and(corner, slab_below), (slab_after, grp))
     greet(jnp.logical_and(corner, slab_above), (slab_before, grp))
 
@@ -156,6 +184,7 @@
         return sum(flag.astype(jnp.int32) for flag in flags)
 
     peers = count(has_prev, has_next)
+    peers = peers + count(far) + 2 * turns * count(first)
     peers = peers + count(corner) * (1 + count(slab_below, slab_above))
     load_first.wait()
     pl.semaphore_wait(barrier, peers)
@@ -210,10 +239,22 @@
     def _():
         to_prev.start()
 
+    @pl.when(far)
+    def _():
+        raw_aside().start()
+
     @pl.when(inner)
     def _():
-        for j in reversed(range(rows - 1)):
+        for j in reversed(range(1, rows - 1)):
             raw_copy(j).start()
+
+    @pl.when(inner_near)
+    def _():
+        raw_copy(0).start()
+
+    @pl.when(far)
+    def _():
+        raw_straight().start()
 
     @pl.when(has_prev)
     def _():
@@ -256,6 +297,15 @@
     load_lower.wait()
     lax.fori_loop(0, rows, scale_own, 0)
 
+    def help_all():
+        for turn in range(turns):
+            remote(
+                aside.at[turn], aside.at[turn], sem.at[SEND_ASIDE], aside_recv.at[turn], nxt
+            ).wait_recv()
+            help_on(turn).start()
+
+    only(first, help_all)
+
     below = row_id > col_id
 
     def dot(x, y):
@@ -275,19 +325,19 @@
     def pack(w, j, block):
         top, corner = block[0:half, 0:half], block[half:size, half:size]
         both = jnp.where(above, top.astype(F32), corner.astype(F32).T)
-        w[reach + j, 0:half, 0:half] = both.astype(BF16)
-        w[reach + j, 0:half, half:size] = block[0:half, half:size]
-        w[reach + j, half:packed, :] = jnp.broadcast_to(diagonal_of(block), (TILE, size)).astype(BF16)
+        w[reach + j, diag : diag + half, 0:half] = both.astype(BF16)
+        w[reach + j, diag : diag + half, half:size] = block[0:half, half:size]
+        w[reach + j, diag + half : tall, :] = jnp.broadcast_to(diagonal_of(block), (TILE, size)).astype(BF16)
 
     def unpack(w, d, j):
-        both = w[j, 0:half, 0:half].astype(F32)
-        diagonal = w[j, half:packed, :].astype(F32)[0:1]
+        both = w[j, diag : diag + half, 0:half].astype(F32)
+        diagonal = w[j, diag + half : tall, :].astype(F32)[0:1]
         on = eye[0:half, 0:half]
         for n, part in enumerate((both, both.T)):
             place = slice(n * half, (n + 1) * half)
             value = jnp.where(above, part, 0.0) + jnp.where(on, diagonal[:, place], 0.0)
             d[j, place, place] = value.astype(BF16)
-        d[j, 0:half, half:size] = w[j, 0:half, half:size]
+        d[j, 0:half, half:size] = w[j, diag : diag + half, half:size]
 
     def update(j, low, w, d, put, before_diagonal, after_upper, wait_piece):
         def partial(k, most):
@@ -331,8 +381,7 @@
 
         @pl.when(from_edge)
         def _():
-            for way, part in enumerate(way_rows):
-                remote(w1.at[j, part], w1.at[j, part], row_send.at[1], recv1.at[j, way], nxt).wait_recv()
+            remote(w1.at[j], w1.at[j], sem.at[SEND_ROWS], recv1.at[j], nxt).wait_recv()
             unpack(w1, d1, j)
 
         @pl.when(from_inner)
@@ -368,7 +417,7 @@
 
         @pl.when(inner)
         def _():
-            start([row_copy(j, n) for n in range(3)])
+            start([row_copy(j, n) for n in range(2)])
 
         @pl.when(edge)
         def _():
@@ -393,7 +442,7 @@
         def before_diagonal():
             @pl.when(from_edge)
             def _():
-                row_copy(j, 3).wait_recv()
+                row_copy(j, 2).wait_recv()
 
         def after_upper():
             def send():
@@ -406,10 +455,10 @@
             pass_on(1, j)
 
         def wait_piece(k):
-            if k != 1:
+            if k in (0, reach - 1):
                 @pl.when(has_prev)
                 def _():
-                    row_copy(j, max(k - 1, 0)).wait_recv()
+                    row_copy(j, 1 if k else 0).wait_recv()
                     if k == 0:
                         unpack(w2, d2, j)
 
@@ -427,25 +476,30 @@
     @pl.when(inner)
     def _():
         raw = blk.at[:, pl.ds(reach, reach + 1)]
-        remote(raw, h1, row_send.at[0], recv1.at[0, 0], nxt).wait_send()
+        remote(raw, h1, sem.at[SEND_RAW], recv1.at[0], nxt).wait_send()
 
     lax.fori_loop(0, rows, second_sweep, 0)
 
     @pl.when(inner)
     def _():
-        part = w2.at[pl.ds(reach, rows), pl.ds(0, packed + (reach - 1) * size)]
-        remote(part, part, row_send.at[1], recv2.at[0, 0], nxt).wait_send()
+        part = w2.at[pl.ds(reach, rows), pl.ds(size, tall - size)]
+        remote(part, part, sem.at[SEND_ROWS], recv2.at[0, 0], nxt).wait_send()
 
     def sent_edge():
         for t, w in enumerate((w2, w1)):
             part = w.at[pl.ds(reach, rows)]
-            remote(part, part, row_send.at[1 - t], recv2.at[0, 0], nxt).wait_send()
+            remote(part, part, sem.at[SEND_RAW if t else SEND_ROWS], recv2.at[0, 0], nxt).wait_send()
 
     only(edge, sent_edge)
+
+    def helped():
+        remote(aside, aside, sem.at[SEND_ASIDE], recv2.at[0, 0], nxt).wait_send()
+
+    only(first, helped)
     for way, duty in enumerate((by_last, by_first)):
         def passed():
             part = relay.at[:, :, way_rows[way]]
-            remote(part, part, relay_send.at[0], recv2.at[0, 0], nxt).wait_send()
+            remote(part, part, sem.at[RELAYED], recv2.at[0, 0], nxt).wait_send()
 
         only(duty, passed)
 
@@ -468,6 +522,7 @@
         scratch_shapes=[
             pltpu.VMEM(blocks.shape, BF16),
             pltpu.VMEM((2, rows, packed + 2 * size, size), BF16),
+            pltpu.VMEM((groups // SPAN - 1,) + block, BF16),
             pltpu.SMEM((2, rows), jnp.int32),
             pltpu.VMEM((rows, 1, size), F32),
             pltpu.VMEM((AUX, size), F32),
@@ -482,8 +537,8 @@
             pltpu.VMEM((rows, reach) + block, BF16),
             pltpu.VMEM((rows, reach + 1) + block, BF16),
             pltpu.VMEM((reach - 1,) + block, F32),
-            dma((5,)), dma((4,)), dma((2,)), dma((rows, 2)), dma((rows, 4)),
-            dma((2, rows, 2)), dma((1,)),
+            dma((6,)), dma((2,)), dma((rows,)), dma((rows, 3)), dma((2, rows, 2)),
+            dma((groups // SPAN - 1,)),
         ],
         compiler_params=pltpu.CompilerParams(collective_id=0, has_side_effects=True, vmem_limit_bytes=57 << 20),
     )(blocks, shift, offsets.T)

time: 55.3 us -> 54.1 us (0.978)
  Pallas kernels: 53 us -> 51.3 us
    pallas_call x1, Pallas kernels: 53 us -> 51.3 us  [per_device(): pl.pallas_call(functools.partial(kernel, slabs, groups, reach), out_shape...]
where the time goes in v4:
time: 54.1 us; the launch traced here: 53.5 us
  Pallas kernels  51.3 us (95%)
  local copies, waits for them, and re-layouts  2.19 us (4%)
    pallas_call x1, Pallas kernels, per_device(): pl.pallas_call(functools.partial(kernel, slabs, groups, reach), out_shape...  51.3 us
    unnamed x1, local copies, waits for them, and re-layouts  2.19 us

profile of v4, /device:TPU:8, one launch (start us, length us, event | category | flops | bytes accessed | tf_op | source)
XLA Modules:
  0.0 53.5 jit_solution(2464934970423476314)
XLA Ops:
  0.0 51.3 %shard_map.37 = bf16[4,9,256,256]{3,2,1,0:T(8,128)(2,1)S(1)} custom-call(bf16[4,9,256,256]{3,2,1,0:T(8,128)(2,1)} %blocks.1, f32[4,1,256]{2,1,0:T(1,128)} %bitcast.2, s32[2,4]{1,0:T(2,128)} %bitcast.3), custom_call_target="tpu_custom_call" | custom-call | tf_op jit(solution)/shard_map/pallas_call | solution.py:517
  51.3 2.2 %copy.5 = bf16[4,9,256,256]{3,2,1,0:T(8,128)(2,1)} copy(bf16[4,9,256,256]{3,2,1,0:T(8,128)(2,1)S(1)} %shard_map.37) | data formatting | bytes 9437184

commit v5 on v4

--- a/solution.py
+++ b/solution.py
@@ -11,7 +11,7 @@
 F32 = jnp.float32
 BF16 = jnp.bfloat16
 
-DIAG, SHIFT, RIGHT, LEFT, AUX = 0, 4, 8, 12, 16
+DIAG, RIGHT, LEFT, SENT, AUX = 0, 4, 8, 8, 16
 TILE = 8
 LOAD_FIRST, LOAD_UPPER, LOAD_LOWER, LOAD_SHIFT, LOAD_OFFSETS = range(5)
 SEND_RAW, SEND_NEXT, RELAYED, SEND_ROWS, SEND_PREV, SEND_ASIDE = range(6)
@@ -50,14 +50,14 @@
     diag = reach * size
     tall = diag + packed
 
-    def cut(n):
-        return pl.ds(2 * size, 2 * size + packed) if n == 0 else pl.ds((2 - n) * size, size)
+    whole = pl.ds(0, tall)
+    most = pl.ds(size, tall - size)
+    near, third = pl.ds(2 * size, 2 * size + packed), pl.ds(size, size)
 
     def upper(s):
         return pl.ds((reach - s) * size, size)
 
-    ways = ((0,), (1, 2))
-    way_rows = (pl.ds(0, packed + 2 * size), pl.ds(0, 2 * size))
+    ways = (near, pl.ds(0, 2 * size))
 
     def remote(src, dst, send, recv, device):
         return pltpu.make_async_remote_copy(
@@ -80,35 +80,29 @@
 
         lax.fori_loop(0, jnp.where(flag, 1, 0), run, 0)
 
-    def slot(t, j, n):
-        return relay.at[t, j, way_rows[0] if n == 0 else pl.ds((n - 1) * size, size)]
+    def slot(t, j, way):
+        return relay.at[t, j, pl.ds(0, ways[way].size)]
 
     def edge_copies(t, j):
         src, send = (w1, sem.at[SEND_RAW]) if t else (w2, sem.at[SEND_ROWS])
         return [
-            remote(src.at[reach + j, cut(n)], slot(t, j, n), send, relay_recv.at[t, j, i], device)
-            for way, device in zip(ways, ((slab_after, groups - 1), (slab, 0)))
-            for i, n in enumerate(way)
+            remote(src.at[reach + j, ways[way]], slot(t, j, way), send, relay_recv.at[t, j], device)
+            for way, device in enumerate(((slab_after, groups - 1), (slab, 0)))
         ]
 
     def forward(t, j, way):
-        device = (slab, 0) if way == 0 else (slab_after, 0)
-        return [
-            remote(
-                slot(t, j, n), (w2 if t else w1).at[j, cut(n)], sem.at[RELAYED],
-                recv2.at[j, n] if t else recv1.at[j], device,
-            )
-            for n in ways[way]
-        ]
+        return remote(
+            slot(t, j, way), (w2 if t else w1).at[j, ways[way]], sem.at[RELAYED],
+            (recv2 if t else recv1).at[j], (slab, 0) if way == 0 else (slab_after, 0),
+        )
 
     def pass_on(t, j):
         for way, duty in enumerate((by_last, by_first)):
             def go():
-                for i, (n, copy) in enumerate(zip(ways[way], forward(t, j, way))):
-                    remote(
-                        slot(t, j, n), slot(t, j, n), sem.at[RELAYED], relay_recv.at[t, j, i], nxt
-                    ).wait_recv()
-                    copy.start()
+                remote(
+                    slot(t, j, way), slot(t, j, way), sem.at[RELAYED], relay_recv.at[t, j], nxt
+                ).wait_recv()
+                forward(t, j, way).start()
 
             only(duty, go)
 
@@ -125,7 +119,7 @@
     def raw_aside():
         turn = lax.div(grp, SPAN)
         return remote(
-            blk.at[0, 2 * reach], aside.at[turn], sem.at[SEND_RAW], aside_recv.at[turn], (slab, 0)
+            blk.at[0, 2 * reach], aside.at[turn], sem.at[SEND_RAW], aside_recv.at[0], (slab, 0)
         )
 
     def raw_straight():
@@ -139,8 +133,8 @@
             aside.at[turn], h1.at[0, reach], sem.at[SEND_ASIDE], recv1.at[0], (slab, SPAN * (turn + 1))
         )
 
-    def row_copy(j, n):
-        return remote(w2.at[reach + j, cut(n)], w2.at[j, cut(n)], sem.at[SEND_ROWS], recv2.at[j, n], nxt)
+    def row_copy(j, part, arrived):
+        return remote(w2.at[reach + j, part], w2.at[j, part], sem.at[SEND_ROWS], recv2.at[arrived], nxt)
 
     def load(which, rows_of, cut_of):
         return pltpu.make_async_copy(
@@ -154,8 +148,8 @@
     load_shift = pltpu.make_async_copy(shifts, shift_own, sem.at[LOAD_SHIFT])
     load_offsets = pltpu.make_async_copy(offsets_in, offsets, sem.at[LOAD_OFFSETS])
 
-    to_next = remote(aux_own, aux_prev, sem.at[SEND_NEXT], aux_recv.at[0], nxt)
-    to_prev = remote(aux_own.at[pl.ds(0, 8)], aux_next, sem.at[SEND_PREV], aux_recv.at[1], prv)
+    to_next = remote(aux_own.at[pl.ds(0, SENT)], aux_prev, sem.at[SEND_NEXT], aux_recv.at[0], nxt)
+    to_prev = remote(aux_own.at[pl.ds(0, SENT)], aux_next, sem.at[SEND_PREV], aux_recv.at[1], prv)
 
     barrier = pltpu.get_barrier_semaphore()
 
@@ -224,7 +218,6 @@
             jnp.where(eye, blk[j, reach].astype(F32), 0.0), axis=0, keepdims=True
         )
         aux_own[DIAG + j : DIAG + j + 1, :] = shift_own[j] + diagonal
-        aux_own[SHIFT + j : SHIFT + j + 1, :] = shift_own[j]
         row = here * rows + j
         right = jnp.minimum(offsets[1, j], slabs * groups * rows - 1 - row)
         left = jnp.minimum(offsets[0, j], row)
@@ -273,10 +266,10 @@
         place, away = (RIGHT, k - reach) if k >= reach else (LEFT, reach - k)
         return table[pl.ds(place + j, 1), :] >= away
 
-    def scaled_block(block, table, j, k, shift, left, right):
+    def scaled_block(block, table, j, k, left, right):
         value = block.astype(F32)
         if k == reach:
-            value = value + jnp.where(eye, shift, 0.0)
+            value = jnp.where(eye, table[pl.ds(DIAG + j, 1), :], value)
         value = value * left * right
         if k != reach:
             value = jnp.where(mask_of(table, j, k), value, 0.0)
@@ -284,9 +277,8 @@
 
     def scale_own(j, carry):
         left = as_column(scale[rows + j])
-        shift = aux_own[pl.ds(SHIFT + j, 1), :]
         for k in range(band):
-            value = scaled_block(blk[j, k], aux_own, j, k, shift, left, scale[j + k])
+            value = scaled_block(blk[j, k], aux_own, j, k, left, scale[j + k])
             a[j, k] = value
             if k == reach:
                 d1[reach + j] = value
@@ -298,10 +290,8 @@
     lax.fori_loop(0, rows, scale_own, 0)
 
     def help_all():
+        remote(aside, aside, sem.at[SEND_ASIDE], aside_recv.at[0], nxt).wait_recv()
         for turn in range(turns):
-            remote(
-                aside.at[turn], aside.at[turn], sem.at[SEND_ASIDE], aside_recv.at[turn], nxt
-            ).wait_recv()
             help_on(turn).start()
 
     only(first, help_all)
@@ -388,10 +378,9 @@
         def _():
             raw_copy(j).wait_recv()
             left = as_column(scale[j])
-            shift = aux_prev[pl.ds(SHIFT + j, 1), :]
             for k in range(reach + 1):
                 value = scaled_block(
-                    h1[j, k], aux_prev, j, reach + k, shift, left, scale[j + k]
+                    h1[j, k], aux_prev, j, reach + k, left, scale[j + k]
                 )
                 if k == 0:
                     d1[j] = value
@@ -417,7 +406,12 @@
 
         @pl.when(inner)
         def _():
-            start([row_copy(j, n) for n in range(2)])
+            for copy, now in (
+                (row_copy(j, most, j), j > 0),
+                (row_copy(j, near, j), j == 0),
+                (row_copy(j, third, rows), j == 0),
+            ):
+                pl.when(now)(copy.start)
 
         @pl.when(edge)
         def _():
@@ -442,7 +436,8 @@
         def before_diagonal():
             @pl.when(from_edge)
             def _():
-                row_copy(j, 2).wait_recv()
+                row_copy(j, whole, j).wait_recv()
+                unpack(w2, d2, j)
 
         def after_upper():
             def send():
@@ -455,12 +450,15 @@
             pass_on(1, j)
 
         def wait_piece(k):
-            if k in (0, reach - 1):
-                @pl.when(has_prev)
+            if k == 0:
+                @pl.when(from_inner)
                 def _():
-                    row_copy(j, 1 if k else 0).wait_recv()
-                    if k == 0:
-                        unpack(w2, d2, j)
+                    pl.when(j > 0)(row_copy(j, most, j).wait_recv)
+                    pl.when(j == 0)(row_copy(j, near, j).wait_recv)
+                    unpack(w2, d2, j)
+
+            if k == reach - 1:
+                pl.when(jnp.logical_and(from_inner, j == 0))(row_copy(j, third, rows).wait_recv)
 
         update(j, low2, w2, d2, put, before_diagonal, after_upper, wait_piece)
         return carry
@@ -482,24 +480,24 @@
 
     @pl.when(inner)
     def _():
-        part = w2.at[pl.ds(reach, rows), pl.ds(size, tall - size)]
-        remote(part, part, sem.at[SEND_ROWS], recv2.at[0, 0], nxt).wait_send()
+        part = w2.at[pl.ds(reach, rows), most]
+        remote(part, part, sem.at[SEND_ROWS], recv2.at[0], nxt).wait_send()
 
     def sent_edge():
         for t, w in enumerate((w2, w1)):
             part = w.at[pl.ds(reach, rows)]
-            remote(part, part, sem.at[SEND_RAW if t else SEND_ROWS], recv2.at[0, 0], nxt).wait_send()
+            remote(part, part, sem.at[SEND_RAW if t else SEND_ROWS], recv2.at[0], nxt).wait_send()
 
     only(edge, sent_edge)
 
     def helped():
-        remote(aside, aside, sem.at[SEND_ASIDE], recv2.at[0, 0], nxt).wait_send()
+        remote(aside, aside, sem.at[SEND_ASIDE], recv2.at[0], nxt).wait_send()
 
     only(first, helped)
     for way, duty in enumerate((by_last, by_first)):
         def passed():
-            part = relay.at[:, :, way_rows[way]]
-            remote(part, part, sem.at[RELAYED], recv2.at[0, 0], nxt).wait_send()
+            part = relay.at[:, :, pl.ds(0, ways[way].size)]
+            remote(part, part, sem.at[RELAYED], recv2.at[0], nxt).wait_send()
 
         only(duty, passed)
 
@@ -526,8 +524,8 @@
             pltpu.SMEM((2, rows), jnp.int32),
             pltpu.VMEM((rows, 1, size), F32),
             pltpu.VMEM((AUX, size), F32),
-            pltpu.VMEM((AUX, size), F32),
-            pltpu.VMEM((8, size), F32),
+            pltpu.VMEM((SENT, size), F32),
+            pltpu.VMEM((SENT, size), F32),
             pltpu.VMEM((3 * rows, 1, size), F32),
             pltpu.VMEM(blocks.shape, BF16),
             pltpu.VMEM(tall, BF16),
@@ -537,8 +535,7 @@
             pltpu.VMEM((rows, reach) + block, BF16),
             pltpu.VMEM((rows, reach + 1) + block, BF16),
             pltpu.VMEM((reach - 1,) + block, F32),
-            dma((6,)), dma((2,)), dma((rows,)), dma((rows, 3)), dma((2, rows, 2)),
-            dma((groups // SPAN - 1,)),
+            dma((6,)), dma((2,)), dma((rows,)), dma((rows + 1,)), dma((2, rows)), dma((1,)),
         ],
         compiler_params=pltpu.CompilerParams(collective_id=0, has_side_effects=True, vmem_limit_bytes=57 << 20),
     )(blocks, shift, offsets.T)

time: 54.1 us -> 53.9 us (level)
  no operation moved by 1% of the time
where the time goes in v5:
time: 53.9 us; the launch traced here: 53.3 us
  Pallas kernels  51.1 us (95%)
  local copies, waits for them, and re-layouts  2.19 us (4%)
    pallas_call x1, Pallas kernels, per_device(): pl.pallas_call(functools.partial(kernel, slabs, groups, reach), out_shape...  51.1 us
    unnamed x1, local copies, waits for them, and re-layouts  2.19 us

profile of v5, /device:TPU:8, one launch (start us, length us, event | category | flops | bytes accessed | tf_op | source)
XLA Modules:
  0.0 53.3 jit_solution(7400733699570967155)
XLA Ops:
  0.0 51.1 %shard_map.37 = bf16[4,9,256,256]{3,2,1,0:T(8,128)(2,1)S(1)} custom-call(bf16[4,9,256,256]{3,2,1,0:T(8,128)(2,1)} %blocks.1, f32[4,1,256]{2,1,0:T(1,128)} %bitcast.2, s32[2,4]{1,0:T(2,128)} %bitcast.3), custom_call_target="tpu_custom_call" | custom-call | tf_op jit(solution)/shard_map/pallas_call | solution.py:515
  51.1 2.2 %copy.5 = bf16[4,9,256,256]{3,2,1,0:T(8,128)(2,1)} copy(bf16[4,9,256,256]{3,2,1,0:T(8,128)(2,1)S(1)} %shard_map.37) | data formatting | bytes 9437184

commit v6 on v5

--- a/solution.py
+++ b/solution.py
@@ -13,16 +13,17 @@
 
 DIAG, RIGHT, LEFT, SENT, AUX = 0, 4, 8, 8, 16
 TILE = 8
-LOAD_FIRST, LOAD_UPPER, LOAD_LOWER, LOAD_SHIFT, LOAD_OFFSETS = range(5)
-SEND_RAW, SEND_NEXT, RELAYED, SEND_ROWS, SEND_PREV, SEND_ASIDE = range(6)
+LOAD_FIRST, LOAD_ROW, LOAD_LOWER, LOAD_SHIFT, LOAD_OFFSETS, LOAD_UPPER, LOAD_REST = range(7)
+SEND_RAW, SEND_NEXT, RELAYED, SEND_ROWS, SEND_PREV, SEND_ASIDE, SEND_EARLY = range(7)
+EARLY = 2
 SPAN = 4
 
 
 def kernel(
     slabs, groups, reach,
     blocks, shifts, offsets_in, f2,
-    blk, relay, aside, offsets, shift_own, aux_own, aux_prev, aux_next, scale, a, w1, w2, d1, d2, low2, h1, acc,
-    sem, aux_recv, recv1, recv2, relay_recv, aside_recv,
+    blk, relay, aside, early, offsets, shift_own, aux_own, aux_prev, aux_next, scale, a, w1, w2, d1, d2, low2, h1, acc,
+    sem, aux_recv, recv1, recv2, relay_recv, aside_recv, early_recv, ready,
 ):
     rows, band, size, _ = blk.shape
     slab, grp = lax.axis_index("slab"), lax.axis_index("grp")
@@ -114,7 +115,21 @@
     turns = aside.shape[0]
     far = jnp.logical_and(lax.rem(grp, SPAN) == SPAN - 1, inner)
     from_far = jnp.logical_and(lax.rem(grp, SPAN) == 0, grp > 0)
-    inner_near = jnp.logical_and(inner, jnp.logical_not(far))
+    odd = lax.rem(grp, 2) == 1
+    even = jnp.logical_not(odd)
+    odd_inner, even_inner = jnp.logical_and(odd, inner), jnp.logical_and(even, inner)
+    odd_near = jnp.logical_and(odd_inner, jnp.logical_not(far))
+    hands_early = jnp.logical_and(odd, grp > 2)
+    here_on = pl.ds(0, EARLY)
+    odd_after = (slab, lax.rem(grp + 2, groups))
+
+    def raw_early():
+        return remote(
+            blk.at[0, pl.ds(reach, EARLY)], early, sem.at[SEND_RAW], early_recv.at[0], odd_after
+        )
+
+    def early_on():
+        return remote(early, h1.at[0, here_on], sem.at[SEND_EARLY], recv1.at[0], prv)
 
     def raw_aside():
         turn = lax.div(grp, SPAN)
@@ -122,10 +137,10 @@
             blk.at[0, 2 * reach], aside.at[turn], sem.at[SEND_RAW], aside_recv.at[0], (slab, 0)
         )
 
-    def raw_straight():
-        part = pl.ds(0, reach)
+    def raw_straight(blocks_left):
         return remote(
-            blk.at[0, pl.ds(reach, reach)], h1.at[0, part], sem.at[SEND_RAW], recv1.at[0], nxt
+            blk.at[0, pl.ds(reach + EARLY, blocks_left)], h1.at[0, pl.ds(EARLY, blocks_left)],
+            sem.at[SEND_RAW], recv1.at[0], nxt,
         )
 
     def help_on(turn):
@@ -142,8 +157,10 @@
         )
 
     above_cut = pl.ds(reach, reach + 1)
-    load_first = load(LOAD_FIRST, pl.ds(rows - 1, 1), above_cut)
-    load_upper = load(LOAD_UPPER, pl.ds(0, rows - 1), above_cut)
+    load_first = load(LOAD_FIRST, pl.ds(0, 1), pl.ds(reach, EARLY))
+    load_row = load(LOAD_ROW, pl.ds(rows - 1, 1), above_cut)
+    load_upper = load(LOAD_UPPER, pl.ds(1, rows - 2), above_cut)
+    load_rest = load(LOAD_REST, pl.ds(0, 1), pl.ds(reach + EARLY, reach + 1 - EARLY))
     load_lower = load(LOAD_LOWER, pl.ds(0, rows), pl.ds(0, reach))
     load_shift = pltpu.make_async_copy(shifts, shift_own, sem.at[LOAD_SHIFT])
     load_offsets = pltpu.make_async_copy(offsets_in, offsets, sem.at[LOAD_OFFSETS])
@@ -158,30 +175,55 @@
         def _():
             pl.semaphore_signal(barrier, inc=1, device_id=device, device_id_type=MESH)
 
-    corner = jnp.logical_and(jnp.logical_or(first, last), slabs > 1)
-    greet(has_prev, prv)
-    greet(has_next, nxt)
-    greet(corner, (slab, groups - 1 - grp))
-    greet(jnp.logical_or(far, from_far), (slab, 0))
-    for turn in range(turns):
-        greet(first, (slab, SPAN * turn + SPAN - 1))
-    greet(jnp.logical_and(corner, slab_below), (slab_after, grp))
-    greet(jnp.logical_and(corner, slab_above), (slab_before, grp))
+    def tell(flag, n, device):
+        @pl.when(flag)
+        def _():
+            pl.semaphore_signal(ready.at[n], inc=1, device_id=device, device_id_type=MESH)
+
+    both = jnp.logical_and
+    corner = both(jnp.logical_or(first, last), slabs > 1)
+    greet(hands_early, (slab, lax.rem(grp + groups - 2, groups)))
+    greet(both(odd, has_next), nxt)
+    greet(odd, prv)
 
     load_first.start()
+    load_row.start()
     load_shift.start()
     load_offsets.start()
     load_upper.start()
+    load_rest.start()
     load_lower.start()
+
+    greet(both(last, slabs > 1), (slab, 0))
+    greet(both(corner, slab_below), (slab_after, grp))
+    greet(both(corner, slab_above), (slab_before, grp))
+    greet(jnp.logical_or(far, from_far), (slab, 0))
 
     def count(*flags):
         return sum(flag.astype(jnp.int32) for flag in flags)
 
-    peers = count(has_prev, has_next)
-    peers = peers + count(far) + 2 * turns * count(first)
-    peers = peers + count(corner) * (1 + count(slab_below, slab_above))
-    load_first.wait()
+    around = count(corner) * count(slab_below, slab_above)
+    mine = count(odd_inner) + around
+    theirs = count(has_prev) + 1 + count(both(first, slabs > 1)) + around + 2 * turns * count(first)
+    peers = jnp.where(odd, mine, theirs)
     pl.semaphore_wait(barrier, peers)
+
+    @pl.when(odd_inner)
+    def _():
+        load_first.wait()
+        raw_early().start()
+
+    tell(both(even, has_prev), 0, prv)
+    tell(even, 2, nxt)
+    tell(both(first, slabs > 1), 2, (slab, groups - 1))
+    for turn in range(turns):
+        tell(first, 1, (slab, SPAN * turn + SPAN - 1))
+    pl.when(jnp.logical_not(odd_inner))(load_first.wait)
+    load_row.wait()
+
+    @pl.when(both(odd, has_next))
+    def _():
+        pl.semaphore_wait(ready.at[0], 1)
 
     @pl.when(inner)
     def _():
@@ -213,6 +255,7 @@
     load_shift.wait()
     load_offsets.wait()
     load_upper.wait()
+    load_rest.wait()
     for j in range(rows):
         diagonal = jnp.sum(
             jnp.where(eye, blk[j, reach].astype(F32), 0.0), axis=0, keepdims=True
@@ -228,26 +271,30 @@
     def _():
         to_next.start()
 
-    @pl.when(has_prev)
-    def _():
-        to_prev.start()
-
-    @pl.when(far)
-    def _():
-        raw_aside().start()
-
     @pl.when(inner)
     def _():
         for j in reversed(range(1, rows - 1)):
             raw_copy(j).start()
 
-    @pl.when(inner_near)
+    @pl.when(even_inner)
     def _():
         raw_copy(0).start()
 
+    @pl.when(odd_near)
+    def _():
+        raw_straight(reach + 1 - EARLY).start()
+
     @pl.when(far)
     def _():
-        raw_straight().start()
+        raw_straight(reach - EARLY).start()
+
+    @pl.when(odd)
+    def _():
+        pl.semaphore_wait(ready.at[2], 1 + count(both(last, slabs > 1)))
+
+    @pl.when(has_prev)
+    def _():
+        to_prev.start()
 
     @pl.when(has_prev)
     def _():
@@ -288,6 +335,11 @@
 
     load_lower.wait()
     lax.fori_loop(0, rows, scale_own, 0)
+
+    @pl.when(far)
+    def _():
+        pl.semaphore_wait(ready.at[1], 1)
+        raw_aside().start()
 
     def help_all():
         remote(aside, aside, sem.at[SEND_ASIDE], aside_recv.at[0], nxt).wait_recv()
@@ -421,6 +473,12 @@
 
     lax.fori_loop(0, rows, first_sweep, 0)
 
+    def hand_early():
+        remote(early, early, sem.at[SEND_EARLY], early_recv.at[0], nxt).wait_recv()
+        early_on().start()
+
+    only(hands_early, hand_early)
+
     def pass_first(i, carry):
         pass_on(0, rows - 1 - i)
         return carry
@@ -494,6 +552,10 @@
         remote(aside, aside, sem.at[SEND_ASIDE], recv2.at[0], nxt).wait_send()
 
     only(first, helped)
+
+    @pl.when(hands_early)
+    def _():
+        early_on().wait_send()
     for way, duty in enumerate((by_last, by_first)):
         def passed():
             part = relay.at[:, :, pl.ds(0, ways[way].size)]
@@ -521,6 +583,7 @@
             pltpu.VMEM(blocks.shape, BF16),
             pltpu.VMEM((2, rows, packed + 2 * size, size), BF16),
             pltpu.VMEM((groups // SPAN - 1,) + block, BF16),
+            pltpu.VMEM((EARLY,) + block, BF16),
             pltpu.SMEM((2, rows), jnp.int32),
             pltpu.VMEM((rows, 1, size), F32),
             pltpu.VMEM((AUX, size), F32),
@@ -535,7 +598,8 @@
             pltpu.VMEM((rows, reach) + block, BF16),
             pltpu.VMEM((rows, reach + 1) + block, BF16),
             pltpu.VMEM((reach - 1,) + block, F32),
-            dma((6,)), dma((2,)), dma((rows,)), dma((rows + 1,)), dma((2, rows)), dma((1,)),
+            dma((7,)), dma((2,)), dma((rows,)), dma((rows + 1,)), dma((2, rows)), dma((1,)),
+            dma((1,)), pltpu.SemaphoreType.REGULAR((3,)),
         ],
         compiler_params=pltpu.CompilerParams(collective_id=0, has_side_effects=True, vmem_limit_bytes=57 << 20),
     )(blocks, shift, offsets.T)

time: 53.9 us -> 53.4 us (level)
  Pallas kernels: 51.1 us -> 50.5 us
where the time goes in v6:
time: 53.4 us; the launch traced here: 52.7 us
  Pallas kernels  50.5 us (95%)
  local copies, waits for them, and re-layouts  2.19 us (4%)
    pallas_call x1, Pallas kernels, per_device(): pl.pallas_call(functools.partial(kernel, slabs, groups, reach), out_shape...  50.5 us
    unnamed x1, local copies, waits for them, and re-layouts  2.19 us

profile of v6, /device:TPU:8, one launch (start us, length us, event | category | flops | bytes accessed | tf_op | source)
XLA Modules:
  0.0 52.7 jit_solution(13244109038027853085)
XLA Ops:
  0.0 50.5 %shard_map.37 = bf16[4,9,256,256]{3,2,1,0:T(8,128)(2,1)S(1)} custom-call(bf16[4,9,256,256]{3,2,1,0:T(8,128)(2,1)} %blocks.1, f32[4,1,256]{2,1,0:T(1,128)} %bitcast.2, s32[2,4]{1,0:T(2,128)} %bitcast.3), custom_call_target="tpu_custom_call" | custom-call | tf_op jit(solution)/shard_map/pallas_call | solution.py:577
  50.6 2.2 %copy.5 = bf16[4,9,256,256]{3,2,1,0:T(8,128)(2,1)} copy(bf16[4,9,256,256]{3,2,1,0:T(8,128)(2,1)S(1)} %shard_map.37) | data formatting | bytes 9437184

commit v7 on v6

--- a/solution.py
+++ b/solution.py
@@ -58,7 +58,8 @@
     def upper(s):
         return pl.ds((reach - s) * size, size)
 
-    ways = (near, pl.ds(0, 2 * size))
+    middle = tall // 32 * 16
+    ways = (pl.ds(middle, tall - middle), pl.ds(0, middle))
 
     def remote(src, dst, send, recv, device):
         return pltpu.make_async_remote_copy(

time: 53.4 us -> 53.4 us (level)
  no operation moved by 1% of the time
where the time goes in v7:
time: 53.4 us; the launch traced here: 52.7 us
  Pallas kernels  50.5 us (95%)
  local copies, waits for them, and re-layouts  2.19 us (4%)
    pallas_call x1, Pallas kernels, per_device(): pl.pallas_call(functools.partial(kernel, slabs, groups, reach), out_shape...  50.5 us
    unnamed x1, local copies, waits for them, and re-layouts  2.19 us

profile of v7, /device:TPU:8, one launch (start us, length us, event | category | flops | bytes accessed | tf_op | source)
XLA Modules:
  0.0 52.7 jit_solution(7129468928548644163)
XLA Ops:
  0.0 50.5 %shard_map.37 = bf16[4,9,256,256]{3,2,1,0:T(8,128)(2,1)S(1)} custom-call(bf16[4,9,256,256]{3,2,1,0:T(8,128)(2,1)} %blocks.1, f32[4,1,256]{2,1,0:T(1,128)} %bitcast.2, s32[2,4]{1,0:T(2,128)} %bitcast.3), custom_call_target="tpu_custom_call" | custom-call | tf_op jit(solution)/shard_map/pallas_call | solution.py:578
  50.6 2.2 %copy.5 = bf16[4,9,256,256]{3,2,1,0:T(8,128)(2,1)} copy(bf16[4,9,256,256]{3,2,1,0:T(8,128)(2,1)S(1)} %shard_map.37) | data formatting | bytes 9437184

commit v8 on v7

--- a/solution.py
+++ b/solution.py
@@ -23,7 +23,7 @@
     slabs, groups, reach,
     blocks, shifts, offsets_in, f2,
     blk, relay, aside, early, offsets, shift_own, aux_own, aux_prev, aux_next, scale, a, w1, w2, d1, d2, low2, h1, acc,
-    sem, aux_recv, recv1, recv2, relay_recv, aside_recv, early_recv, ready,
+    sem, aux_recv, recv1, recv2, relay_recv, side_recv, ready,
 ):
     rows, band, size, _ = blk.shape
     slab, grp = lax.axis_index("slab"), lax.axis_index("grp")
@@ -126,7 +126,7 @@
 
     def raw_early():
         return remote(
-            blk.at[0, pl.ds(reach, EARLY)], early, sem.at[SEND_RAW], early_recv.at[0], odd_after
+            blk.at[0, pl.ds(reach, EARLY)], early, sem.at[SEND_RAW], side_recv.at[0], odd_after
         )
 
     def early_on():
@@ -135,7 +135,7 @@
     def raw_aside():
         turn = lax.div(grp, SPAN)
         return remote(
-            blk.at[0, 2 * reach], aside.at[turn], sem.at[SEND_RAW], aside_recv.at[0], (slab, 0)
+            blk.at[0, 2 * reach], aside.at[turn], sem.at[SEND_RAW], side_recv.at[0], (slab, 0)
         )
 
     def raw_straight(blocks_left):
@@ -343,7 +343,7 @@
         raw_aside().start()
 
     def help_all():
-        remote(aside, aside, sem.at[SEND_ASIDE], aside_recv.at[0], nxt).wait_recv()
+        remote(aside, aside, sem.at[SEND_ASIDE], side_recv.at[0], nxt).wait_recv()
         for turn in range(turns):
             help_on(turn).start()
 
@@ -475,7 +475,7 @@
     lax.fori_loop(0, rows, first_sweep, 0)
 
     def hand_early():
-        remote(early, early, sem.at[SEND_EARLY], early_recv.at[0], nxt).wait_recv()
+        remote(early, early, sem.at[SEND_EARLY], side_recv.at[0], nxt).wait_recv()
         early_on().start()
 
     only(hands_early, hand_early)
@@ -600,7 +600,7 @@
             pltpu.VMEM((rows, reach + 1) + block, BF16),
             pltpu.VMEM((reach - 1,) + block, F32),
             dma((7,)), dma((2,)), dma((rows,)), dma((rows + 1,)), dma((2, rows)), dma((1,)),
-            dma((1,)), pltpu.SemaphoreType.REGULAR((3,)),
+            pltpu.SemaphoreType.REGULAR((3,)),
         ],
         compiler_params=pltpu.CompilerParams(collective_id=0, has_side_effects=True, vmem_limit_bytes=57 << 20),
     )(blocks, shift, offsets.T)

time: 53.4 us -> 53.4 us (level)
  no operation moved by 1% of the time
where the time goes in v8:
time: 53.4 us; the launch traced here: 52.7 us
  Pallas kernels  50.5 us (95%)
  local copies, waits for them, and re-layouts  2.19 us (4%)
    pallas_call x1, Pallas kernels, per_device(): pl.pallas_call(functools.partial(kernel, slabs, groups, reach), out_shape...  50.5 us
    unnamed x1, local copies, waits for them, and re-layouts  2.19 us

profile of v8, /device:TPU:8, one launch (start us, length us, event | category | flops | bytes accessed | tf_op | source)
XLA Modules:
  0.0 52.7 jit_solution(17882958510108128571)
XLA Ops:
  0.0 50.5 %shard_map.37 = bf16[4,9,256,256]{3,2,1,0:T(8,128)(2,1)S(1)} custom-call(bf16[4,9,256,256]{3,2,1,0:T(8,128)(2,1)} %blocks.1, f32[4,1,256]{2,1,0:T(1,128)} %bitcast.2, s32[2,4]{1,0:T(2,128)} %bitcast.3), custom_call_target="tpu_custom_call" | custom-call | tf_op jit(solution)/shard_map/pallas_call | solution.py:578
  50.5 2.2 %copy.5 = bf16[4,9,256,256]{3,2,1,0:T(8,128)(2,1)} copy(bf16[4,9,256,256]{3,2,1,0:T(8,128)(2,1)S(1)} %shard_map.37) | data formatting | bytes 9437184
